TPU v7x, 256 devices: a whole 4x4x8 slice. The times are simulated.
256 devices in a mesh: grp: 4 (over x), hold: 64 (over y, z, core).
Axes of the slice: x: 4, y: 4, z: 8, core: 2. Of those that a mesh axis runs over, the one named last changes fastest.
Arguments:
- queries: bfloat16 [256, 4096], P(('grp', 'hold')), may hold values from -60 to 60
- prefix_len: int32 [256], P(('grp', 'hold')), may hold values from 128 to 65536
- prefix_keys: bfloat16 [512, 128, 2048], P(('grp', 'hold')), may hold values from -15 to 15
- prefix_values: bfloat16 [512, 128, 2048], P(('grp', 'hold')), may hold values from -24 to 24
- block_table: int32 [512], P(('grp', 'hold')), may hold values from 0 to 511, each once
- suffix_keys: bfloat16 [256, 128, 2048], P(('grp', 'hold')), may hold values from -15 to 15
- suffix_values: bfloat16 [256, 128, 2048], P(('grp', 'hold')), may hold values from -24 to 24
Outputs:
- attention: bfloat16 [256, 4096], P(('grp', 'hold'))
- log_normalizer: float32 [256, 32], P(('grp', 'hold'))
All inputs are finite; a program needn't handle non-finite values.
Results may differ from a plain program's by a relative error of at most 0.0035.
Values may be sent and summed in bfloat16 or wider, within the bound.
A program may use at most 64 MiB of HBM per device.

v0:
```python
import math

import jax
import jax.numpy as jnp
from jax import lax
from jax.sharding import Mesh
from jax.sharding import PartitionSpec as P

HEADS = 32
KV_HEADS = 16
HEAD_DIM = 128
GRP_HOLD = ("grp", "hold_0", "hold_1", "hold_2")


score_scale = 1.0 / 168.0**0.5
masked_score = -1e30


def sent_to_all(x, axis):
    devices = lax.axis_size(axis)
    return lax.all_to_all(jnp.broadcast_to(x[None], (devices, *x.shape)), axis, 0, 0, tiled=True)


def joined_along(parts, dim):
    parts = jnp.moveaxis(parts, 0, dim)
    shape = parts.shape
    return parts.reshape(*shape[:dim], shape[dim] * shape[dim + 1], *shape[dim + 2 :])


def whole_of(x, axes, dim):
    far, near = axes
    parts = sent_to_all(sent_to_all(x, far), near)
    return joined_along(parts.swapaxes(0, 1).reshape(-1, *x.shape), dim)


def of_everyone(x, axis):
    everything = sent_to_all(x, axis)
    return jnp.max(everything, axis=0)


def by_axis(x, axes):
    far, near = axes
    nearer = of_everyone(x, near)
    return of_everyone(nearer, far)


def split_up(x, dim, devices):
    before, after = (x.shape[:dim], x.shape[dim + 1 :])
    return jnp.moveaxis(x.reshape(*before, devices, -1, *after), dim, 0)


def summed_on_arrival(x, axis, dim):
    parts = split_up(x, dim, lax.axis_size(axis))
    arrived = lax.all_to_all(parts, axis, split_axis=0, concat_axis=0, tiled=True)
    return arrived.sum(axis=0)


def sum_in_two_steps(x, axes, dim):
    far, near = axes
    initial = summed_on_arrival(x, far, dim)
    return summed_on_arrival(initial, near, dim)


def combine_parts(first, second):
    top = jnp.maximum(first[0], second[0])
    left = jnp.exp(first[0] - top)
    right = jnp.exp(second[0] - top)
    return (
        top,
        first[1] * left + second[1] * right,
        first[2] * left[..., None] + second[2] * right[..., None],
    )


def prefix_partials(query_rows, lengths, keys, values, table):
    count = query_rows.shape[0]
    blocks, block_len, width = keys.shape
    group = HEADS // KV_HEADS
    keys_heads = keys.reshape(blocks, block_len, KV_HEADS, HEAD_DIM)
    values_heads = values.reshape(blocks, block_len, KV_HEADS, HEAD_DIM)
    positions = table[:, None] * block_len + jnp.arange(block_len, dtype=jnp.int32)[None, :]
    row_block = math.gcd(count, max(1, 32768 // (blocks * block_len)))

    def per_rows(pair):
        query_block, length_block = pair
        query_heads = query_block.reshape(row_block, KV_HEADS, group, HEAD_DIM)
        scores = (
            jnp.einsum(
                "rgqd,btgd->rgqbt", query_heads, keys_heads, preferred_element_type=jnp.float32
            )
            * score_scale
        )
        live = (positions[None, :, :] < length_block[:, None, None])[:, None, None, :, :]
        scores = jnp.where(live, scores, masked_score)
        block_max = jnp.max(scores, axis=-1)
        weights = jnp.where(live, jnp.exp(scores - block_max[..., None]), 0.0).astype(jnp.bfloat16)
        block_sum = jnp.sum(weights.astype(jnp.float32), axis=-1)
        block_out = jnp.einsum(
            "rgqbt,btgd->rgqbd", weights, values_heads, preferred_element_type=jnp.float32
        )
        local_max = jnp.max(block_max, axis=-1)
        factor = jnp.exp(block_max - local_max[..., None])
        local_sum = jnp.sum(block_sum * factor, axis=-1)
        local_out = jnp.sum(block_out * factor[..., None], axis=-2)
        return (
            local_max.reshape(row_block, HEADS),
            local_sum.reshape(row_block, HEADS),
            local_out.reshape(row_block, HEADS, HEAD_DIM),
        )

    turns = count // row_block
    pieces = lax.map(
        per_rows, (query_rows.reshape(turns, row_block, -1), lengths.reshape(turns, row_block))
    )
    return tuple((piece.reshape((count,) + piece.shape[2:]) for piece in pieces))


def suffix_partials(queries, suffix_keys, suffix_values):
    count, length, width = suffix_keys.shape
    group = HEADS // KV_HEADS
    query_heads = queries.reshape(count, KV_HEADS, group, HEAD_DIM)
    keys_heads = suffix_keys.reshape(count, length, KV_HEADS, HEAD_DIM)
    values_heads = suffix_values.reshape(count, length, KV_HEADS, HEAD_DIM)
    scores = (
        jnp.einsum("rgqd,rtgd->rgqt", query_heads, keys_heads, preferred_element_type=jnp.float32)
        * score_scale
    )
    block_max = jnp.max(scores, axis=-1)
    weights = jnp.exp(scores - block_max[..., None]).astype(jnp.bfloat16)
    block_sum = jnp.sum(weights.astype(jnp.float32), axis=-1)
    block_out = jnp.einsum(
        "rgqt,rtgd->rgqd", weights, values_heads, preferred_element_type=jnp.float32
    )
    return (
        block_max.reshape(count, HEADS),
        block_sum.reshape(count, HEADS),
        block_out.reshape(count, HEADS, HEAD_DIM),
    )


def body(queries, prefix_len, prefix_keys, prefix_values, block_table, suffix_keys, suffix_values):
    count = queries.shape[0]
    rows_all, lengths_all = (
        whole_of(queries, ("grp", ("hold_0", "hold_1", "hold_2")), 0),
        whole_of(prefix_len, ("grp", ("hold_0", "hold_1", "hold_2")), 0),
    )
    pieces = prefix_partials(rows_all, lengths_all, prefix_keys, prefix_values, block_table)
    start = lax.axis_index(GRP_HOLD) * count
    peak = by_axis(
        pieces[0].astype(jnp.bfloat16), (("grp", "hold_0"), ("hold_1", "hold_2"))
    ).astype(jnp.float32)
    factor = jnp.exp(pieces[0] - peak)
    totals = (
        sum_in_two_steps(pieces[1] * factor, ("grp", ("hold_0", "hold_1", "hold_2")), 0),
        sum_in_two_steps(pieces[2] * factor[..., None], ("grp", ("hold_0", "hold_1", "hold_2")), 0),
    )
    prefix = (lax.dynamic_slice_in_dim(peak, start, count, 0), totals[0], totals[1])
    private = suffix_partials(queries, suffix_keys, suffix_values)
    top, normalizer, numerator = combine_parts(prefix, private)
    attention = (
        (numerator / normalizer[..., None]).reshape(count, HEADS * HEAD_DIM).astype(jnp.bfloat16)
    )
    log_normalizer = top + jnp.log(normalizer)
    return (attention, log_normalizer)


def solution(mesh):
    split = Mesh(
        mesh.devices.reshape(mesh.shape["grp"], 4, 8, 2), ("grp", "hold_0", "hold_1", "hold_2")
    )
    in_specs = (
        P(GRP_HOLD, None),
        P(GRP_HOLD),
        P(GRP_HOLD, None, None),
        P(GRP_HOLD, None, None),
        P(GRP_HOLD),
        P(GRP_HOLD, None, None),
        P(GRP_HOLD, None, None),
    )
    out_specs = (P(GRP_HOLD, None), P(GRP_HOLD, None))
    return jax.shard_map(body, mesh=split, in_specs=in_specs, out_specs=out_specs, check_vma=False)
```

profile of v0, /device:TPU:1, one launch (start us, length us, event | category | flops | bytes accessed | tf_op | source)
XLA Modules:
  0.0 267.6 jit_solution(4504677246205814647)
XLA Ops:
  2.0 4.8 %all-to-all-start = ((s32[4,1,1]{2,1,0:T(1,128)}), s32[4,1,1]{2,1,0:T(1,128)S(1)}, u32[]{:S(2)}, u32[]{:S(2)}) async-start(s32[4,1,1]{2,1,0:T(1,128)} %broadcast_in_dim.93), calls=%async_computation | async-start | bytes 4096 | tf_op jit(solution)/shard_map/all_to_all | solution.py:21
  10.8 3.3 %all-to-all-start.2 = ((bf16[4,2,2048]{2,1,0:T(2,128)(2,1)}), bf16[4,2,2048]{2,1,0:T(2,128)(2,1)S(1)}, u32[]{:S(2)}, u32[]{:S(2)}) async-start(bf16[4,2,2048]{2,1,0:T(2,128)(2,1)} %reshape.255), calls=%async_computation.2 | async-start | bytes 65536 | tf_op jit(solution)/shard_map/all_to_all | solution.py:21
  14.3 4.1 %all-to-all-done.2 = bf16[4,2,2048]{2,1,0:T(2,128)(2,1)S(1)} async-done(((bf16[4,2,2048]{2,1,0:T(2,128)(2,1)}), bf16[4,2,2048]{2,1,0:T(2,128)(2,1)S(1)}, u32[]{:S(2)}, u32[]{:S(2)}) %all-to-all-start.2) | async-done | bytes 32800 | tf_op jit(solution)/shard_map/all_to_all | solution.py:21
  19.0 14.9 %all-to-all-start.1 = ((s32[64,4,1]{1,2,0:T(1,128)}), s32[64,4,1]{1,2,0:T(1,128)S(1)}, u32[]{:S(2)}, u32[]{:S(2)}) async-start(s32[64,4,1]{1,2,0:T(1,128)} %broadcast_in_dim.95), calls=%async_computation.1 | async-start | bytes 65536 | tf_op jit(solution)/shard_map/all_to_all | solution.py:21
  34.0 9.2 %all-to-all-done.1 = s32[64,4,1]{1,2,0:T(1,128)S(1)} async-done(((s32[64,4,1]{1,2,0:T(1,128)}), s32[64,4,1]{1,2,0:T(1,128)S(1)}, u32[]{:S(2)}, u32[]{:S(2)}) %all-to-all-start.1) | async-done | bytes 1056 | tf_op jit(solution)/shard_map/all_to_all | solution.py:21
  43.2 2.4 broadcast_in_dim.99
  45.6 5.7 %all-to-all-start.3 = ((bf16[64,4,1,4096]{3,1,2,0:T(4,128)(2,1)}), bf16[64,4,1,4096]{3,1,2,0:T(4,128)(2,1)}, u32[]{:S(2)}, u32[]{:S(2)}) async-start(bf16[64,4,1,4096]{3,1,2,0:T(4,128)(2,1)} %broadcast_in_dim.99), calls=%async_computation.3 | async-start | bytes 4194304 | tf_op jit(solution)/shard_map/all_to_all | solution.py:21
  55.5 47.0 %all-to-all-done.3 = bf16[64,4,1,4096]{3,1,2,0:T(4,128)(2,1)} async-done(((bf16[64,4,1,4096]{3,1,2,0:T(4,128)(2,1)}), bf16[64,4,1,4096]{3,1,2,0:T(4,128)(2,1)}, u32[]{:S(2)}, u32[]{:S(2)}) %all-to-all-start.3) | async-done | bytes 2097184 | tf_op jit(solution)/shard_map/all_to_all | solution.py:21
  102.5 2.7 %copy.114 = bf16[64,4,1,4096]{3,0,1,2:T(8,128)(2,1)S(1)} copy(bf16[64,4,1,4096]{3,1,2,0:T(4,128)(2,1)} %all-to-all-done.3) | data formatting | bytes 4194304 | tf_op jit(solution)/shard_map/all_to_all | solution.py:21
  105.3 22.9 %while.15 = (s32[]{:T(128)}, f32[2,128,32]{1,2,0:T(8,128)S(1)}, f32[2,128,32]{1,0,2:T(2,128)S(1)}, f32[2,128,32,128]{3,2,1,0:T(8,128)}, s32[2,128]{1,0:T(2,128)S...) while((s32[]{:T(128)}, f32[2,128,32]{1,2,0:T(8,128)S(1)}, ...), condition=%wide.region_6.7_spmd.clone, body=%wide.region_0.6_spmd.clone.sunk | while | flops 550011136 | bytes 81252120 | solution.py:112
  107.4 2.1 bitcast_reduce_fusion.4
  109.6 1.5 convert_reduce_fusion.3
  111.2 2.0 fusion.31
  113.4 1.4 copy_dynamic-update-slice_fusion.2
  114.8 1.9 copy-done.3
  118.8 2.1 bitcast_reduce_fusion.4
  121.0 1.5 convert_reduce_fusion.3
  122.7 2.0 fusion.31
  124.8 1.4 copy_dynamic-update-slice_fusion.2
  126.2 1.9 copy-done.3
  128.2 15.8 %all_to_all.51 = bf16[16,256,32]{1,2,0:T(8,128)(2,1)S(1)} all-to-all(bf16[16,256,32]{1,2,0:T(8,128)(2,1)S(1)} %broadcast_in_dim.100), channel_id=1, replica_groups=mesh['grp'=4,'hold_0'=4,'hold_1'=8,'hold_2'=2] {'hold_1','hold_2'}, dimensions={0} | all-to-all | bytes 524288 | tf_op jit(solution)/shard_map/all_to_all | solution.py:21
  144.8 3.7 %all-to-all-start.5 = ((bf16[16,256,32]{1,2,0:T(8,128)(2,1)}), bf16[16,256,32]{1,2,0:T(8,128)(2,1)S(1)}, u32[]{:S(2)}, u32[]{:S(2)}) async-start(bf16[16,256,32]{1,2,0:T(8,128)(2,1)} %broadcast_in_dim.101), calls=%async_computation.5 | async-start | bytes 524288 | tf_op jit(solution)/shard_map/all_to_all | solution.py:21
  148.8 8.0 %all-to-all-done.5 = bf16[16,256,32]{1,2,0:T(8,128)(2,1)S(1)} async-done(((bf16[16,256,32]{1,2,0:T(8,128)(2,1)}), bf16[16,256,32]{1,2,0:T(8,128)(2,1)S(1)}, u32[]{:S(2)}, u32[]{:S(2)}) %all-to-all-start.5) | async-done | bytes 262176 | tf_op jit(solution)/shard_map/all_to_all | solution.py:21
  157.7 3.3 %all-to-all-start.8 = ((f32[4,1,2048]{2,1,0:T(1,128)}), f32[4,1,2048]{2,1,0:T(1,128)S(1)}, u32[]{:S(2)}, u32[]{:S(2)}) async-start(f32[4,1,2048]{2,1,0:T(1,128)} %reshape.257), calls=%async_computation.8 | async-start | bytes 65536 | tf_op jit(solution)/shard_map/all_to_all | solution.py:54
  161.1 4.2 %broadcast_multiply_fusion = f32[4,64,32,128]{3,2,1,0:T(8,128)} fusion(f32[4,64,32,128]{3,2,1,0:T(8,128)} %bitcast.114, f32[4,64,32]{2,1,0:T(8,128)S(1)} %copy.123), kind=kLoop, calls=%fused_computation.24 | loop fusion | flops 1048576 | bytes 8421376 | tf_op jit(solution)/shard_map/mul | solution.py:155
  165.2 4.9 %all-to-all-start.6 = ((f32[4,64,32,128]{3,2,1,0:T(8,128)}), f32[4,64,32,128]{3,2,1,0:T(8,128)}, u32[]{:S(2)}, u32[]{:S(2)}) async-start(f32[4,64,32,128]{3,2,1,0:T(8,128)} %broadcast_multiply_fusion), calls=%async_computation.6 | async-start | bytes 8388608 | tf_op jit(solution)/shard_map/all_to_all | solution.py:54
  172.2 44.7 %all-to-all-done.6 = f32[4,64,32,128]{3,2,1,0:T(8,128)} async-done(((f32[4,64,32,128]{3,2,1,0:T(8,128)}), f32[4,64,32,128]{3,2,1,0:T(8,128)}, u32[]{:S(2)}, u32[]{:S(2)}) %all-to-all-start.6) | async-done | bytes 4194336 | tf_op jit(solution)/shard_map/all_to_all | solution.py:54
  216.8 7.0 %all-to-all-start.9 = ((f32[64,1,32]{2,1,0:T(1,128)}), f32[64,1,32]{2,1,0:T(1,128)S(1)}, u32[]{:S(2)}, u32[]{:S(2)}) async-start(f32[64,1,32]{2,1,0:T(1,128)} %copy.131), calls=%async_computation.9 | async-start | bytes 65536 | tf_op jit(solution)/shard_map/all_to_all | solution.py:54
  223.9 3.8 %reduce_sum.76 = f32[64,32,128]{2,1,0:T(8,128)} reduce(f32[4,64,32,128]{3,2,1,0:T(8,128)} %all-to-all-done.6, f32[]{:T(128)} %constant.19.clone.1), dimensions={0}, to_apply=%region_9.10 | reduce | flops 786432 | bytes 5242884 | tf_op jit(solution)/shard_map/reduce_sum | solution.py:55
  227.7 5.6 %all-to-all-done.9 = f32[64,1,32]{2,1,0:T(1,128)S(1)} async-done(((f32[64,1,32]{2,1,0:T(1,128)}), f32[64,1,32]{2,1,0:T(1,128)S(1)}, u32[]{:S(2)}, u32[]{:S(2)}) %all-to-all-start.9) | async-done | bytes 8224 | tf_op jit(solution)/shard_map/all_to_all | solution.py:54
  233.3 4.8 %all-to-all-start.7 = ((f32[64,1,32,128]{3,2,1,0:T(8,128)}), f32[64,1,32,128]{3,2,1,0:T(8,128)S(1)}, u32[]{:S(2)}, u32[]{:S(2)}) async-start(f32[64,1,32,128]{3,2,1,0:T(8,128)} %bitcast.7), calls=%async_computation.7 | async-start | bytes 2097152 | tf_op jit(solution)/shard_map/all_to_all | solution.py:54
  240.6 26.1 %all-to-all-done.7 = f32[64,1,32,128]{3,2,1,0:T(8,128)S(1)} async-done(((f32[64,1,32,128]{3,2,1,0:T(8,128)}), f32[64,1,32,128]{3,2,1,0:T(8,128)S(1)}, u32[]{:S(2)}, u32[]{:S(2)}) %all-to-all-start.7) | async-done | bytes 1048608 | tf_op jit(solution)/shard_map/all_to_all | solution.py:54
  (104 shorter events, 21.8 us)
Async XLA Ops:
  0.6 50.7 %copy-start.4 = (bf16[2,128,2048]{2,1,0:T(8,128)(2,1)S(1)}, bf16[2,128,2048]{2,1,0:T(8,128)(2,1)}, u32[]{:S(2)}) copy-start(bf16[2,128,2048]{2,1,0:T(8,128)(2,1)} %param.11) | copy-start | bytes 3145732
  2.0 8.9 %all-to-all-start = ((s32[4,1,1]{2,1,0:T(1,128)}), s32[4,1,1]{2,1,0:T(1,128)S(1)}, u32[]{:S(2)}, u32[]{:S(2)}) async-start(s32[4,1,1]{2,1,0:T(1,128)} %broadcast_in_dim.93), calls=%async_computation | async-start | bytes 4096 | tf_op jit(solution)/shard_map/all_to_all | solution.py:21
  10.8 7.5 %all-to-all-start.2 = ((bf16[4,2,2048]{2,1,0:T(2,128)(2,1)}), bf16[4,2,2048]{2,1,0:T(2,128)(2,1)S(1)}, u32[]{:S(2)}, u32[]{:S(2)}) async-start(bf16[4,2,2048]{2,1,0:T(2,128)(2,1)} %reshape.255), calls=%async_computation.2 | async-start | bytes 65536 | tf_op jit(solution)/shard_map/all_to_all | solution.py:21
  19.0 24.2 %all-to-all-start.1 = ((s32[64,4,1]{1,2,0:T(1,128)}), s32[64,4,1]{1,2,0:T(1,128)S(1)}, u32[]{:S(2)}, u32[]{:S(2)}) async-start(s32[64,4,1]{1,2,0:T(1,128)} %broadcast_in_dim.95), calls=%async_computation.1 | async-start | bytes 65536 | tf_op jit(solution)/shard_map/all_to_all | solution.py:21
  45.6 7.8 %copy-start.5 = (bf16[2,128,2048]{2,1,0:T(8,128)(2,1)S(1)}, bf16[2,128,2048]{2,1,0:T(8,128)(2,1)}, u32[]{:S(2)}) copy-start(bf16[2,128,2048]{2,1,0:T(8,128)(2,1)} %param.12) | copy-start | bytes 3145732
  45.6 56.9 %all-to-all-start.3 = ((bf16[64,4,1,4096]{3,1,2,0:T(4,128)(2,1)}), bf16[64,4,1,4096]{3,1,2,0:T(4,128)(2,1)}, u32[]{:S(2)}, u32[]{:S(2)}) async-start(bf16[64,4,1,4096]{3,1,2,0:T(4,128)(2,1)} %broadcast_in_dim.99), calls=%async_computation.3 | async-start | bytes 4194304 | tf_op jit(solution)/shard_map/all_to_all | solution.py:21
  51.3 4.0 %copy-start.9 = (s32[2]{0:T(128)S(1)}, s32[2]{0:T(128)}, u32[]{:S(2)}) copy-start(s32[2]{0:T(128)} %param.13) | copy-start | bytes 28
  105.3 1.3 copy-start
  109.5 1.7 copy-start.6
  111.2 2.2 copy-start.2
  113.3 3.5 %copy-start.1 = (bf16[2,128,4096]{2,1,0:T(8,128)(2,1)S(1)}, bf16[2,128,4096]{2,1,0:T(8,128)(2,1)}, u32[]{:S(2)}) copy-start(bf16[2,128,4096]{2,1,0:T(8,128)(2,1)} %copy-done) | copy-start | bytes 6291460 | tf_op jit(solution)/shard_map/while
  114.8 1.9 copy-start.3
  116.7 1.3 copy-start
  121.0 1.7 copy-start.6
  122.6 2.2 copy-start.2
  124.7 3.5 %copy-start.1 = (bf16[2,128,4096]{2,1,0:T(8,128)(2,1)S(1)}, bf16[2,128,4096]{2,1,0:T(8,128)(2,1)}, u32[]{:S(2)}) copy-start(bf16[2,128,4096]{2,1,0:T(8,128)(2,1)} %copy-done) | copy-start | bytes 6291460 | tf_op jit(solution)/shard_map/while
  126.2 1.9 copy-start.3
  144.8 12.0 %all-to-all-start.5 = ((bf16[16,256,32]{1,2,0:T(8,128)(2,1)}), bf16[16,256,32]{1,2,0:T(8,128)(2,1)S(1)}, u32[]{:S(2)}, u32[]{:S(2)}) async-start(bf16[16,256,32]{1,2,0:T(8,128)(2,1)} %broadcast_in_dim.101), calls=%async_computation.5 | async-start | bytes 524288 | tf_op jit(solution)/shard_map/all_to_all | solution.py:21
  157.7 7.6 %all-to-all-start.8 = ((f32[4,1,2048]{2,1,0:T(1,128)}), f32[4,1,2048]{2,1,0:T(1,128)S(1)}, u32[]{:S(2)}, u32[]{:S(2)}) async-start(f32[4,1,2048]{2,1,0:T(1,128)} %reshape.257), calls=%async_computation.8 | async-start | bytes 65536 | tf_op jit(solution)/shard_map/all_to_all | solution.py:54
  165.2 51.6 %all-to-all-start.6 = ((f32[4,64,32,128]{3,2,1,0:T(8,128)}), f32[4,64,32,128]{3,2,1,0:T(8,128)}, u32[]{:S(2)}, u32[]{:S(2)}) async-start(f32[4,64,32,128]{3,2,1,0:T(8,128)} %broadcast_multiply_fusion), calls=%async_computation.6 | async-start | bytes 8388608 | tf_op jit(solution)/shard_map/all_to_all | solution.py:54
  170.1 68.0 %copy-start.7 = (bf16[1,128,2048]{2,1,0:T(8,128)(2,1)S(1)}, bf16[1,128,2048]{2,1,0:T(8,128)(2,1)}, u32[]{:S(2)}) copy-start(bf16[1,128,2048]{2,1,0:T(8,128)(2,1)} %param.14) | copy-start | bytes 1572868
  216.8 16.5 %all-to-all-start.9 = ((f32[64,1,32]{2,1,0:T(1,128)}), f32[64,1,32]{2,1,0:T(1,128)S(1)}, u32[]{:S(2)}, u32[]{:S(2)}) async-start(f32[64,1,32]{2,1,0:T(1,128)} %copy.131), calls=%async_computation.9 | async-start | bytes 65536 | tf_op jit(solution)/shard_map/all_to_all | solution.py:54
  223.9 15.2 %copy-start.8 = (bf16[1,128,2048]{2,1,0:T(8,128)(2,1)S(1)}, bf16[1,128,2048]{2,1,0:T(8,128)(2,1)}, u32[]{:S(2)}) copy-start(bf16[1,128,2048]{2,1,0:T(8,128)(2,1)} %param.15) | copy-start | bytes 1572868
  233.3 33.4 %all-to-all-start.7 = ((f32[64,1,32,128]{3,2,1,0:T(8,128)}), f32[64,1,32,128]{3,2,1,0:T(8,128)S(1)}, u32[]{:S(2)}, u32[]{:S(2)}) async-start(f32[64,1,32,128]{3,2,1,0:T(8,128)} %bitcast.7), calls=%async_computation.7 | async-start | bytes 2097152 | tf_op jit(solution)/shard_map/all_to_all | solution.py:54
where the time goes:
time: 269 us; the launch traced here: 268 us
  waiting for transfers between devices  146 us (54%)
  starting transfers between devices  52.4 us (19%)
  local copies, waits for them, and re-layouts  27.1 us (10%)
  blocking collectives  15.8 us (6%)
  other arithmetic  15.4 us (6%)
  matrix products  9.09 us (3%)
    all_to_all x4, waiting for transfers between devices, summed_on_arrival(): lax.all_to_all(parts, axis, split_axis=0, concat_axis=0, tiled=True)  76.4 us
    all_to_all x5, waiting for transfers between devices, sent_to_all(): lax.all_to_all(jnp.broadcast_to(x[None], (devices, *x.shape)), axis, 0, 0...  69.6 us
    all_to_all x5, starting transfers between devices, sent_to_all(): lax.all_to_all(jnp.broadcast_to(x[None], (devices, *x.shape)), axis, 0, 0...  32.4 us
    all_to_all x4, starting transfers between devices, summed_on_arrival(): lax.all_to_all(parts, axis, split_axis=0, concat_axis=0, tiled=True)  20 us
    all_to_all x1, blocking collectives, sent_to_all(): lax.all_to_all(jnp.broadcast_to(x[None], (devices, *x.shape)), axis, 0, 0...  15.8 us
    unnamed x22, local copies, waits for them, and re-layouts  6.38 us
    while x20, local copies, waits for them, and re-layouts  6.33 us
  transfers between devices with their start and end apart: 9, of which 8 were waited for; matrix products, arithmetic and copies ran while one was open for 7% of the time, Pallas kernels for 0%

commit v1 on v0

v1 whole, which is shorter than its diff:
```python
import functools
import math

import jax
import jax.numpy as jnp
from jax import lax
from jax.experimental import pallas as pl
from jax.experimental.pallas import tpu as pltpu
from jax.sharding import Mesh
from jax.sharding import PartitionSpec as P

HEADS = 32
KV_HEADS = 16
HEAD_DIM = 128
HALF = HEADS // 2
KV_HALF = KV_HEADS // 2
AXES = ("x", "y", "z", "c")
MESH = pl.DeviceIdType.MESH

SCALE2 = math.log2(math.e) / 168.0**0.5
LN2 = math.log(2.0)
MASKED = -1e30
FLOOR = -1e29

NT = (((1,), (1,)), ((), ()))
NN = (((1,), (0,)), ((), ()))


def kernel(
    q_ref, len_ref, pos_ref, k_ref, v_ref, ks_ref, vs_ref,
    out_ref, log_ref,
    zq, zl, turn, turn2, qg, kbuf, vbuf, pbuf, ksb, vsb,
    osend, msend, orecv, mrecv, osend2, msend2, orecv2, mrecv2, so, sm, sl,
    local_sem, kv_send, kv_recv, zq_send, zq_recv, zl_send, zl_recv,
    xy_send, xy_recv, ro_send, ro_recv, rm_send, rm_recv,
    fo_send, fo_recv, fm_send, fm_recv,
):
    nx, ny, nz = (lax.axis_size(a) for a in AXES[:3])
    x, y, z, c = (lax.axis_index(a) for a in AXES)
    rows = nz * 2
    mine, plane = z * 2 + c, x * ny + y
    other = 1 - c
    width = KV_HALF * HEAD_DIM

    def columns(half):
        return pl.ds(pl.multiple_of(half * width, width), width)

    loads = [
        pltpu.make_async_copy(k_ref.at[:, :, columns(c)], kbuf.at[0], local_sem.at[0]),
        pltpu.make_async_copy(v_ref.at[:, :, columns(c)], vbuf.at[0], local_sem.at[1]),
        pltpu.make_async_copy(ks_ref, ksb, local_sem.at[2]),
        pltpu.make_async_copy(vs_ref, vsb, local_sem.at[3]),
    ]
    for load in loads:
        load.start()

    line = [(dz, dc) for dz in range(nz) for dc in range(2) if (dz, dc) != (0, 0)]
    sheet = [(dx, dy) for dx in range(nx) for dy in range(ny) if (dx, dy) != (0, 0)]

    def line_id(dz, dc):
        return {"z": lax.rem(z + dz, nz), "c": lax.rem(c + dc, 2)}

    def sheet_id(dx, dy):
        return {"x": lax.rem(x + dx, nx), "y": lax.rem(y + dy, ny)}

    barrier = pltpu.get_barrier_semaphore()
    for dz, dc in line:
        pl.semaphore_signal(barrier, inc=1, device_id=line_id(dz, dc), device_id_type=MESH)
    for dx, dy in sheet:
        pl.semaphore_signal(barrier, inc=1, device_id=sheet_id(dx, dy), device_id_type=MESH)
    pl.semaphore_wait(barrier, len(line) + len(sheet))

    def remote(src, dst, send, recv, device):
        return pltpu.make_async_remote_copy(
            src_ref=src, dst_ref=dst, send_sem=send, recv_sem=recv, device_id=device, device_id_type=MESH
        )

    def line_slot(dz, dc):
        return lax.rem(z + nz - dz, nz) * 2 + lax.rem(c + dc, 2)

    def line_gather(dz, dc, slot):
        i, half = dz * 2 + dc, lax.rem(c + dc, 2)
        device = line_id(dz, dc)
        return [
            remote(q_ref.at[half], zq.at[slot], zq_send.at[i], zq_recv.at[i], device),
            remote(len_ref, zl.at[slot], zl_send.at[i], zl_recv.at[i], device),
        ]

    for dz, dc in line:
        for copy in line_gather(dz, dc, mine):
            copy.start()
    partner = {"c": other}
    swaps = [
        remote(pos_ref, pbuf.at[1], kv_send.at[0], kv_recv.at[0], partner),
        remote(k_ref.at[:, :, columns(other)], kbuf.at[1], kv_send.at[1], kv_recv.at[1], partner),
        remote(v_ref.at[:, :, columns(other)], vbuf.at[1], kv_send.at[2], kv_recv.at[2], partner),
    ]
    for copy in swaps:
        copy.start()
    pbuf[0] = pos_ref[...]
    zq[pl.ds(mine, 1)] = q_ref[pl.ds(c, 1)]
    zl[pl.ds(mine, 1)] = len_ref[...][None]

    loads[2].wait()
    loads[3].wait()
    query = q_ref[...].astype(jnp.float32).reshape(HEADS, HEAD_DIM)
    head_kv = lax.broadcasted_iota(jnp.int32, (HEADS, HEAD_DIM), 0) // 2
    own_scores = jnp.zeros((HEADS, 128), jnp.float32)
    for kv in range(KV_HEADS):
        picked = jnp.where(head_kv == kv, query, 0.0).astype(jnp.bfloat16)
        own_scores += lax.dot_general(
            picked, ksb[0, :, kv * HEAD_DIM : (kv + 1) * HEAD_DIM], NT, preferred_element_type=jnp.float32
        )
    own_scores = own_scores * SCALE2
    own_max = jnp.max(own_scores, axis=1, keepdims=True)
    own_weights = jnp.exp2(own_scores - own_max).astype(jnp.bfloat16)
    own_sum = jnp.sum(own_weights.astype(jnp.float32), axis=1, keepdims=True)
    own_out = jnp.zeros((HEADS, HEAD_DIM), jnp.float32)
    for kv in range(KV_HEADS):
        part = lax.dot_general(
            own_weights, vsb[0, :, kv * HEAD_DIM : (kv + 1) * HEAD_DIM], NN, preferred_element_type=jnp.float32
        )
        own_out += jnp.where(head_kv == kv, part, 0.0)
    so[...] = own_out
    sm[...] = jnp.broadcast_to(own_max, (HEADS, 128))
    sl[...] = jnp.broadcast_to(own_sum, (HEADS, 128))

    for dz, dc in line:
        for copy in line_gather(dz, dc, line_slot(dz, dc)):
            copy.wait_recv()
    turn[...] = zq[...].astype(jnp.float32)
    for h in range(HALF):
        qg[pl.ds(plane, 1), h] = turn[:, h, :].astype(jnp.bfloat16)[None]
    length = zl[:, 0, :]
    high = jnp.floor(length * (1.0 / 256.0))
    lane = lax.broadcasted_iota(jnp.int32, (rows, 128), 1)
    qg[pl.ds(plane, 1), HALF] = jnp.where(lane < 64, high, length - high * 256.0).astype(jnp.bfloat16)[None]

    def sheet_gather(i, device, slot):
        return remote(qg.at[plane], qg.at[slot], xy_send.at[i], xy_recv.at[i], device)

    for dx, dy in sheet:
        sheet_gather(dx * ny + dy, sheet_id(dx, dy), plane).start()

    loads[0].wait()
    loads[1].wait()
    for copy in swaps:
        copy.wait_recv()
    positions = jnp.concatenate([pbuf[s, b : b + 1, :] for s in range(2) for b in range(2)], axis=1)
    tokens = 4 * 128
    ones = jnp.ones((tokens, HEAD_DIM), jnp.bfloat16)
    group = ny * 2 * rows

    def sheet_return(i, device, here, there):
        return [
            remote(osend.at[here], orecv.at[there], ro_send.at[i], ro_recv.at[i], device),
            remote(msend.at[here], mrecv.at[there], rm_send.at[i], rm_recv.at[i], device),
        ]

    def chunk(k, carry):
        column = lax.rem(x + k, nx)
        for dy in range(ny):
            row = lax.rem(y + dy, ny)
            back = lax.rem(nx - k, nx) * ny + (ny - dy) % ny

            def arrive(back=back, row=row):
                sheet_gather(back, {"x": column, "y": row}, column * ny + row).wait_recv()

            if dy == 0:
                pl.when(k > 0)(arrive)
            else:
                arrive()
        base = column * ny
        tile = qg[pl.ds(base, ny), HALF].astype(jnp.float32)
        wide = tile[:, :, 0:1] * 256.0 + tile[:, :, 64:65]
        limit = jnp.broadcast_to(wide[:, None], (ny, 2, rows, 1)).reshape(group, 1)
        live = positions < limit
        lanes = lax.broadcasted_iota(jnp.int32, (ny, rows, 128), 2)
        stats = jnp.zeros((ny, rows, 128), jnp.float32)
        for g in range(KV_HALF):
            span = slice(g * HEAD_DIM, (g + 1) * HEAD_DIM)
            queries = qg[pl.ds(base, ny), 2 * g : 2 * g + 2].reshape(group, HEAD_DIM)
            keys = kbuf[:, :, :, span].reshape(tokens, HEAD_DIM)
            values = vbuf[:, :, :, span].reshape(tokens, HEAD_DIM)
            scores = lax.dot_general(queries, keys, NT, preferred_element_type=jnp.float32) * SCALE2
            scores = jnp.where(live, scores, MASKED)
            top = jnp.maximum(jnp.max(scores, axis=1, keepdims=True), FLOOR)
            weights = jnp.exp2(scores - top).astype(jnp.bfloat16)
            both = lax.dot_general(
                weights, jnp.concatenate([values, ones], axis=1), NN, preferred_element_type=jnp.float32
            )
            osend[pl.ds(base, ny), 2 * g : 2 * g + 2] = (
                both[:, :HEAD_DIM].astype(jnp.bfloat16).reshape(ny, 2, rows, HEAD_DIM)
            )
            tops = jnp.broadcast_to(top, (group, 128)).reshape(ny, 2, rows, 128)
            sums = both[:, HEAD_DIM:].reshape(ny, 2, rows, 128)
            for j in range(2):
                stats = jnp.where(lanes == 2 * g + j, tops[:, j], stats)
                stats = jnp.where(lanes == HALF + 2 * g + j, sums[:, j], stats)
        msend[pl.ds(base, ny)] = stats
        for dy in range(ny):
            row = lax.rem(y + dy, ny)
            there = column * ny + row

            def leave(dy=dy, row=row, there=there):
                for copy in sheet_return(k * ny + dy, {"x": column, "y": row}, there, plane):
                    copy.start()

            if dy == 0:
                pl.when(k > 0)(leave)
            else:
                leave()
        return carry

    lax.fori_loop(0, nx, chunk, 0)

    orecv[pl.ds(plane, 1)] = osend[pl.ds(plane, 1)]
    mrecv[pl.ds(plane, 1)] = msend[pl.ds(plane, 1)]
    for dx, dy in sheet:
        slot = lax.rem(x + nx - dx, nx) * ny + lax.rem(y + ny - dy, ny)
        for copy in sheet_return(dx * ny + dy, sheet_id(dx, dy), slot, slot):
            copy.wait_recv()
    count = nx * ny
    best = jnp.max(mrecv[...], axis=0)

    def merge(s, carry):
        total, out = carry
        part = mrecv[pl.ds(s, 1)][0]
        factor = jnp.exp2(part - best)
        total = total + pltpu.roll(factor, HALF, 1) * part
        block = orecv[pl.ds(s, 1)][0].astype(jnp.float32)
        out = tuple(out[h] + factor[:, h : h + 1] * block[h] for h in range(HALF))
        return total, out

    zero = jnp.zeros((rows, HEAD_DIM), jnp.float32)
    total, out = lax.fori_loop(0, count, merge, (zero, (zero,) * HALF))
    msend2[:, 0, :] = jnp.where(lane < HALF, best, total)
    for h in range(HALF):
        turn2[h] = out[h]
    for r in range(rows):
        osend2[r] = turn2[:, r, :].astype(jnp.bfloat16)

    def line_return(dz, dc, here, there):
        i = dz * 2 + dc
        device = line_id(dz, dc)
        return [
            remote(osend2.at[here], orecv2.at[there], fo_send.at[i], fo_recv.at[i], device),
            remote(msend2.at[here], mrecv2.at[there], fm_send.at[i], fm_recv.at[i], device),
        ]

    for dz, dc in line:
        target = lax.rem(z + dz, nz) * 2 + lax.rem(c + dc, 2)
        for copy in line_return(dz, dc, target, mine):
            copy.start()
    orecv2[pl.ds(mine, 1)] = osend2[pl.ds(mine, 1)]
    mrecv2[pl.ds(mine, 1)] = msend2[pl.ds(mine, 1)]
    for dz, dc in line:
        slot = line_slot(dz, dc)
        for copy in line_return(dz, dc, slot, slot):
            copy.wait_recv()

    lane_of = lax.broadcasted_iota(jnp.int32, (HALF, 128), 1)
    head_of = lax.broadcasted_iota(jnp.int32, (HALF, 128), 0)
    for half in range(2):
        heads = slice(half * HALF, (half + 1) * HALF)
        tops, sums = [sm[heads, 0:1]], [sl[heads, 0:1]]
        for s in range(nz):
            row = jnp.broadcast_to(mrecv2[s * 2 + half], (HALF, 128))
            tops.append(jnp.sum(jnp.where(lane_of == head_of, row, 0.0), axis=1, keepdims=True))
            sums.append(jnp.sum(jnp.where(lane_of == head_of + HALF, row, 0.0), axis=1, keepdims=True))
        top = functools.reduce(jnp.maximum, tops)
        factors = [jnp.exp2(t - top) for t in tops]
        normalizer = sum(f * s for f, s in zip(factors, sums))
        numerator = factors[0] * so[heads, :]
        for s in range(nz):
            numerator += factors[s + 1] * orecv2[s * 2 + half].astype(jnp.float32)
        out_ref[heads, :] = (numerator / normalizer).astype(jnp.bfloat16)
        log_ref[heads, :] = jnp.broadcast_to(top * LN2 + jnp.log(normalizer), (HALF, 128))

    for copy in swaps:
        copy.wait_send()
    for dz, dc in line:
        target = lax.rem(z + dz, nz) * 2 + lax.rem(c + dc, 2)
        for copy in line_gather(dz, dc, mine) + line_return(dz, dc, target, mine):
            copy.wait_send()
    for dx, dy in sheet:
        i, device = dx * ny + dy, sheet_id(dx, dy)
        there = lax.rem(x + dx, nx) * ny + lax.rem(y + dy, ny)
        sheet_gather(i, device, plane).wait_send()
        for copy in sheet_return(i, device, there, plane):
            copy.wait_send()


def body(nx, ny, nz, queries, prefix_len, prefix_keys, prefix_values, block_table, suffix_keys, suffix_values):
    rows, count = nz * 2, nx * ny
    q = queries.reshape(2, HALF, HEAD_DIM)
    length = jnp.broadcast_to(prefix_len.astype(jnp.float32)[:, None], (1, 128))
    offsets = jnp.arange(128, dtype=jnp.int32)
    position = (block_table[:, None] * 128 + offsets[None, :]).astype(jnp.float32)
    position = jnp.pad(position, ((0, 6), (0, 0)))
    vmem, hbm = pl.BlockSpec(memory_space=pltpu.VMEM), pl.BlockSpec(memory_space=pl.ANY)
    bf16, f32 = jnp.bfloat16, jnp.float32
    dma = pltpu.SemaphoreType.DMA
    out, logs = pl.pallas_call(
        kernel,
        name="decode",
        out_shape=[
            jax.ShapeDtypeStruct((HEADS, HEAD_DIM), bf16),
            jax.ShapeDtypeStruct((HEADS, 128), f32),
        ],
        in_specs=[vmem, vmem, vmem, hbm, hbm, hbm, hbm],
        out_specs=[vmem, vmem],
        scratch_shapes=[
            pltpu.VMEM((rows, HALF, HEAD_DIM), bf16),
            pltpu.VMEM((rows, 1, 128), f32),
            pltpu.VMEM((rows, HALF, HEAD_DIM), f32),
            pltpu.VMEM((HALF, rows, HEAD_DIM), f32),
            pltpu.VMEM((count, HALF + 1, rows, HEAD_DIM), bf16),
            pltpu.VMEM((2, 2, 128, KV_HALF * HEAD_DIM), bf16),
            pltpu.VMEM((2, 2, 128, KV_HALF * HEAD_DIM), bf16),
            pltpu.VMEM((2, 8, 128), f32),
            pltpu.VMEM((1, 128, KV_HEADS * HEAD_DIM), bf16),
            pltpu.VMEM((1, 128, KV_HEADS * HEAD_DIM), bf16),
            pltpu.VMEM((count, HALF, rows, HEAD_DIM), bf16),
            pltpu.VMEM((count, rows, 128), f32),
            pltpu.VMEM((count, HALF, rows, HEAD_DIM), bf16),
            pltpu.VMEM((count, rows, 128), f32),
            pltpu.VMEM((rows, HALF, HEAD_DIM), bf16),
            pltpu.VMEM((rows, 1, 128), f32),
            pltpu.VMEM((rows, HALF, HEAD_DIM), bf16),
            pltpu.VMEM((rows, 1, 128), f32),
            pltpu.VMEM((HEADS, HEAD_DIM), f32),
            pltpu.VMEM((HEADS, 128), f32),
            pltpu.VMEM((HEADS, 128), f32),
            dma((4,)), dma((3,)), dma((3,)),
            dma((rows,)), dma((rows,)), dma((rows,)), dma((rows,)),
            dma((count,)), dma((count,)),
            dma((count,)), dma((count,)), dma((count,)), dma((count,)),
            dma((rows,)), dma((rows,)), dma((rows,)), dma((rows,)),
        ],
        compiler_params=pltpu.CompilerParams(
            collective_id=0, has_side_effects=True, vmem_limit_bytes=48 * 1024 * 1024
        ),
    )(q, length, position, prefix_keys, prefix_values, suffix_keys, suffix_values)
    return out.reshape(1, HEADS * HEAD_DIM), logs[:, 0].reshape(1, HEADS)


def solution(mesh):
    shape = mesh.shape
    nx = shape["grp"]
    nz = 8 if shape["hold"] == 64 else 2
    ny = shape["hold"] // (2 * nz)
    split = Mesh(mesh.devices.reshape(nx, ny, nz, 2), AXES)
    rows = P(AXES, None)
    return jax.shard_map(
        functools.partial(body, nx, ny, nz),
        mesh=split,
        in_specs=(rows, P(AXES), P(AXES, None, None), P(AXES, None, None), P(AXES), P(AXES, None, None), P(AXES, None, None)),
        out_specs=(rows, rows),
        check_vma=False,
    )
```

time: 269 us -> 67.9 us (0.25)
  waiting for transfers between devices: 146 us -> 0 us
  Pallas kernels: 0 us -> 59.7 us
  starting transfers between devices: 52.4 us -> 0 us
  local copies, waits for them, and re-layouts: 27.1 us -> 5.78 us
  blocking collectives: 15.8 us -> 0 us
  other arithmetic: 15.4 us -> 0.79 us
  matrix products: 9.09 us -> 0 us
    all_to_all x9 -> x0, waiting for transfers between devices: 146 us -> none  [the longest x4 76.4 us: summed_on_arrival(): lax.all_to_all(parts, axis, split_axis=0, concat_axis=0, tiled=True)]
    pallas_call x0 -> x1, Pallas kernels: none -> 59.7 us  [body(): pl.pallas_call(kernel, name='decode', out_shape=[jax.ShapeDtypeStruct((HE...]
    all_to_all x9 -> x0, starting transfers between devices: 52.4 us -> none  [the longest x5 32.4 us: sent_to_all(): lax.all_to_all(jnp.broadcast_to(x[None], (devices, *x.shape)), axis, 0, 0...]
    all_to_all x1 -> x0, blocking collectives: 15.8 us -> none  [sent_to_all(): lax.all_to_all(jnp.broadcast_to(x[None], (devices, *x.shape)), axis, 0, 0...]
    dot_general x6 -> x0, matrix products: 9.09 us -> none  [the longest x2 4.29 us: per_rows(): jnp.einsum('rgqd,btgd->rgqbt', query_heads, keys_heads, preferred_element...]
    reduce_sum x9 -> x0, other arithmetic: 7.25 us -> none  [the longest x4 4 us: summed_on_arrival(): return arrived.sum(axis=0)]
    while x21 -> x0, local copies, waits for them, and re-layouts: 6.36 us -> none
    broadcast_in_dim x7 -> x1, local copies, waits for them, and re-layouts: 4.84 us -> 0.01 us  [body(): length = jnp.broadcast_to(prefix_len.astype(jnp.float32)[:, None], (1, 128))]
  transfers between devices with their start and end apart: 9 -> 0, of which waited for: 8 -> 0; matrix products, arithmetic and copies ran while one was open for 7% -> 0% of each run, Pallas kernels for 0% -> 0%
where the time goes in v1:
time: 67.9 us; the launch traced here: 67.6 us
  Pallas kernels  59.7 us (88%)
  local copies, waits for them, and re-layouts  5.78 us (9%)
  between operations  1.33 us (2%)
  other arithmetic  0.79 us (1%)
    pallas_call x1, Pallas kernels, body(): pl.pallas_call(kernel, name='decode', out_shape=[jax.ShapeDtypeStruct((HE...  59.7 us
    unnamed x11, local copies, waits for them, and re-layouts  5.15 us

profile of v1, /device:TPU:1, one launch (start us, length us, event | category | flops | bytes accessed | tf_op | source)
XLA Modules:
  0.0 67.6 jit_solution(11480967709409191241)
XLA Ops:
  0.6 0.0 copy-start.4
  1.3 0.7 broadcast_multiply_fusion
  2.0 0.1 add_convert_fusion
  2.1 0.0 copy-done.4
  2.1 0.1 reduce
  2.1 0.0 copy-start
  2.1 1.2 %copy-done = bf16[2,128,2048]{2,1,0:T(8,128)(2,1)S(1)} copy-done((bf16[2,128,2048]{2,1,0:T(8,128)(2,1)S(1)}, bf16[2,128,2048]{2,1,0:T(8,128)(2,1)}, u32[]{:S(2)}) %copy-start) | copy-done | bytes 1048600
  3.3 0.0 copy-start.1
  3.3 1.2 %copy-done.1 = bf16[2,128,2048]{2,1,0:T(8,128)(2,1)S(1)} copy-done((bf16[2,128,2048]{2,1,0:T(8,128)(2,1)S(1)}, bf16[2,128,2048]{2,1,0:T(8,128)(2,1)}, u32[]{:S(2)}) %copy-start.1) | copy-done | bytes 1048600
  4.6 0.0 copy-start.2
  4.6 1.0 %copy-done.2 = bf16[1,128,2048]{2,1,0:T(8,128)(2,1)S(1)} copy-done((bf16[1,128,2048]{2,1,0:T(8,128)(2,1)S(1)}, bf16[1,128,2048]{2,1,0:T(8,128)(2,1)}, u32[]{:S(2)}) %copy-start.2) | copy-done | bytes 524312
  5.6 0.0 copy-start.3
  5.6 1.0 %copy-done.3 = bf16[1,128,2048]{2,1,0:T(8,128)(2,1)S(1)} copy-done((bf16[1,128,2048]{2,1,0:T(8,128)(2,1)S(1)}, bf16[1,128,2048]{2,1,0:T(8,128)(2,1)}, u32[]{:S(2)}) %copy-start.3) | copy-done | bytes 524312
  6.6 59.7 %decode.1 = (bf16[32,128]{1,0:T(8,128)(2,1)S(1)}, f32[32,128]{1,0:T(8,128)S(1)}) custom-call(bf16[2,16,128]{2,1,0:T(8,128)(2,1)S(1)} %bitcast.8, f32[1,128]{1,0:T(1,128)S(1)} %broadcast_in_dim.5.len_ref, f32[8,128]{1,0:T(8,128)S(1)} %pad.4.pos_ref, bf16[2,128,2048]{2,1,0:T(8,128)(2,1)S(1)} %copy-done, bf16[2,128,2048]{2,1,0:T(8,128)(2,1)S(1)} %copy-done.1, ...), custom_call_target="tpu_custom_call" | custom-call | tf_op jit(solution)/shard_map/decode/pallas_call | solution.py:304
  66.3 0.6 slice_reduce_fusion
  66.9 0.6 copy.11
  (2 shorter events, 0.0 us)
Async XLA Ops:
  0.6 1.4 %copy-start.4 = (bf16[1,4096]{1,0:T(2,128)(2,1)S(1)}, bf16[1,4096]{1,0:T(2,128)(2,1)}, u32[]{:S(2)}) copy-start(bf16[1,4096]{1,0:T(2,128)(2,1)} %param.7) | copy-start | bytes 24580
  2.1 1.2 %copy-start = (bf16[2,128,2048]{2,1,0:T(8,128)(2,1)S(1)}, bf16[2,128,2048]{2,1,0:T(8,128)(2,1)}, u32[]{:S(2)}) copy-start(bf16[2,128,2048]{2,1,0:T(8,128)(2,1)} %k_ref.1) | copy-start | bytes 3145732
  3.3 1.2 %copy-start.1 = (bf16[2,128,2048]{2,1,0:T(8,128)(2,1)S(1)}, bf16[2,128,2048]{2,1,0:T(8,128)(2,1)}, u32[]{:S(2)}) copy-start(bf16[2,128,2048]{2,1,0:T(8,128)(2,1)} %v_ref.1) | copy-start | bytes 3145732
  4.6 1.0 %copy-start.2 = (bf16[1,128,2048]{2,1,0:T(8,128)(2,1)S(1)}, bf16[1,128,2048]{2,1,0:T(8,128)(2,1)}, u32[]{:S(2)}) copy-start(bf16[1,128,2048]{2,1,0:T(8,128)(2,1)} %ks_ref.1) | copy-start | bytes 1572868
  5.6 1.0 %copy-start.3 = (bf16[1,128,2048]{2,1,0:T(8,128)(2,1)S(1)}, bf16[1,128,2048]{2,1,0:T(8,128)(2,1)}, u32[]{:S(2)}) copy-start(bf16[1,128,2048]{2,1,0:T(8,128)(2,1)} %vs_ref.1) | copy-start | bytes 1572868

commit v2 on v1

--- a/solution.py
+++ b/solution.py
@@ -14,6 +14,7 @@
 HEAD_DIM = 128
 HALF = HEADS // 2
 KV_HALF = KV_HEADS // 2
+FIRST = HALF // 2
 AXES = ("x", "y", "z", "c")
 MESH = pl.DeviceIdType.MESH
 
@@ -27,9 +28,9 @@
 
 
 def kernel(
-    q_ref, len_ref, pos_ref, k_ref, v_ref, ks_ref, vs_ref,
+    flat_ref, len_ref, table_ref, k_ref, v_ref, ks_ref, vs_ref,
     out_ref, log_ref,
-    zq, zl, turn, turn2, qg, kbuf, vbuf, pbuf, ksb, vsb,
+    q_ref, own_len, zq, zl, turn, turn2, qg, kbuf, vbuf, pbuf, ksb, vsb,
     osend, msend, orecv, mrecv, osend2, msend2, orecv2, mrecv2, so, sm, sl,
     local_sem, kv_send, kv_recv, zq_send, zq_recv, zl_send, zl_recv,
     xy_send, xy_recv, ro_send, ro_recv, rm_send, rm_recv,
@@ -54,6 +55,16 @@
     for load in loads:
         load.start()
 
+    flat = flat_ref[...].astype(jnp.float32)
+    for h in range(HEADS):
+        turn2[h % HALF, 0:1, :] = flat[:, h * HEAD_DIM : (h + 1) * HEAD_DIM]
+        if h % HALF == HALF - 1:
+            q_ref[h // HALF] = turn2[:, 0, :].astype(jnp.bfloat16)
+    own_len[...] = jnp.full((1, 128), len_ref[0], jnp.int32).astype(jnp.float32)
+    offset = lax.broadcasted_iota(jnp.int32, (1, 128), 1)
+    for b in range(2):
+        pbuf[0, b : b + 1, :] = (table_ref[b] * 128 + offset).astype(jnp.float32)
+
     line = [(dz, dc) for dz in range(nz) for dc in range(2) if (dz, dc) != (0, 0)]
     sheet = [(dx, dy) for dx in range(nx) for dy in range(ny) if (dx, dy) != (0, 0)]
 
@@ -83,7 +94,7 @@
         device = line_id(dz, dc)
         return [
             remote(q_ref.at[half], zq.at[slot], zq_send.at[i], zq_recv.at[i], device),
-            remote(len_ref, zl.at[slot], zl_send.at[i], zl_recv.at[i], device),
+            remote(own_len, zl.at[slot], zl_send.at[i], zl_recv.at[i], device),
         ]
 
     for dz, dc in line:
@@ -91,15 +102,14 @@
             copy.start()
     partner = {"c": other}
     swaps = [
-        remote(pos_ref, pbuf.at[1], kv_send.at[0], kv_recv.at[0], partner),
+        remote(pbuf.at[0], pbuf.at[1], kv_send.at[0], kv_recv.at[0], partner),
         remote(k_ref.at[:, :, columns(other)], kbuf.at[1], kv_send.at[1], kv_recv.at[1], partner),
         remote(v_ref.at[:, :, columns(other)], vbuf.at[1], kv_send.at[2], kv_recv.at[2], partner),
     ]
     for copy in swaps:
         copy.start()
-    pbuf[0] = pos_ref[...]
     zq[pl.ds(mine, 1)] = q_ref[pl.ds(c, 1)]
-    zl[pl.ds(mine, 1)] = len_ref[...][None]
+    zl[pl.ds(mine, 1)] = own_len[...][None]
 
     loads[2].wait()
     loads[3].wait()
@@ -136,11 +146,35 @@
     lane = lax.broadcasted_iota(jnp.int32, (rows, 128), 1)
     qg[pl.ds(plane, 1), HALF] = jnp.where(lane < 64, high, length - high * 256.0).astype(jnp.bfloat16)[None]
 
-    def sheet_gather(i, device, slot):
-        return remote(qg.at[plane], qg.at[slot], xy_send.at[i], xy_recv.at[i], device)
-
-    for dx, dy in sheet:
-        sheet_gather(dx * ny + dy, sheet_id(dx, dy), plane).start()
+    def sheet_pass(colour, bx, by, dx, dy):
+        tiles = pl.ds(0, FIRST) if colour == 0 else pl.ds(FIRST, HALF + 1 - FIRST)
+        block = lax.rem(x + bx, nx) * ny + lax.rem(y + by, ny)
+        seen = lax.rem(bx + nx - dx, nx) * ny + lax.rem(by + ny - dy, ny)
+        sent = (bx + dx) * ny + dy if colour == 0 else dx * ny + by + dy
+        return remote(
+            qg.at[block, tiles], qg.at[block, tiles],
+            xy_send.at[colour, sent], xy_recv.at[colour, seen], sheet_id(dx, dy),
+        )
+
+    def sheet_arrival(colour, bx, by):
+        tiles = pl.ds(0, FIRST) if colour == 0 else pl.ds(FIRST, HALF + 1 - FIRST)
+        block = qg.at[lax.rem(x + bx, nx) * ny + lax.rem(y + by, ny), tiles]
+        i = bx * ny + by
+        return remote(block, block, xy_send.at[colour, i], xy_recv.at[colour, i], sheet_id(0, 0))
+
+    along_x = [1 + (i // 2 if i % 2 == 0 else nx - 2 - i // 2) for i in range(nx - 1)]
+    along_y = [1 + (i // 2 if i % 2 == 0 else ny - 2 - i // 2) for i in range(ny - 1)]
+    passes = [(0, 0, 0, dx, 0) for dx in along_x] + [(1, 0, 0, 0, dy) for dy in along_y]
+    passes += [(0, 0, 0, 0, dy) for dy in along_y] + [(1, 0, 0, dx, 0) for dx in along_x]
+    for step in passes:
+        sheet_pass(*step).start()
+    seen_first = [(0, bx, 0) for bx in along_x] + [(1, 0, by) for by in along_y]
+    for colour, bx, by in sorted(seen_first, key=lambda b: (along_x + along_y).index(b[1] + b[2])):
+        sheet_arrival(colour, bx, by).wait_recv()
+        onward = [(0, bx, 0, 0, dy) for dy in along_y] if colour == 0 else [(1, 0, by, dx, 0) for dx in along_x]
+        for step in onward:
+            sheet_pass(*step).start()
+        passes += onward
 
     loads[0].wait()
     loads[1].wait()
@@ -159,17 +193,14 @@
 
     def chunk(k, carry):
         column = lax.rem(x + k, nx)
-        for dy in range(ny):
-            row = lax.rem(y + dy, ny)
-            back = lax.rem(nx - k, nx) * ny + (ny - dy) % ny
-
-            def arrive(back=back, row=row):
-                sheet_gather(back, {"x": column, "y": row}, column * ny + row).wait_recv()
-
-            if dy == 0:
-                pl.when(k > 0)(arrive)
-            else:
-                arrive()
+        for dy in range(1, ny):
+            sheet_arrival(0, k, dy).wait_recv()
+
+        def arrive():
+            for dy in range(ny):
+                sheet_arrival(1, k, dy).wait_recv()
+
+        pl.when(k > 0)(arrive)
         base = column * ny
         tile = qg[pl.ds(base, ny), HALF].astype(jnp.float32)
         wide = tile[:, :, 0:1] * 256.0 + tile[:, :, 64:65]
@@ -283,22 +314,18 @@
         target = lax.rem(z + dz, nz) * 2 + lax.rem(c + dc, 2)
         for copy in line_gather(dz, dc, mine) + line_return(dz, dc, target, mine):
             copy.wait_send()
+    for step in passes:
+        sheet_pass(*step).wait_send()
     for dx, dy in sheet:
         i, device = dx * ny + dy, sheet_id(dx, dy)
         there = lax.rem(x + dx, nx) * ny + lax.rem(y + dy, ny)
-        sheet_gather(i, device, plane).wait_send()
         for copy in sheet_return(i, device, there, plane):
             copy.wait_send()
 
 
 def body(nx, ny, nz, queries, prefix_len, prefix_keys, prefix_values, block_table, suffix_keys, suffix_values):
     rows, count = nz * 2, nx * ny
-    q = queries.reshape(2, HALF, HEAD_DIM)
-    length = jnp.broadcast_to(prefix_len.astype(jnp.float32)[:, None], (1, 128))
-    offsets = jnp.arange(128, dtype=jnp.int32)
-    position = (block_table[:, None] * 128 + offsets[None, :]).astype(jnp.float32)
-    position = jnp.pad(position, ((0, 6), (0, 0)))
-    vmem, hbm = pl.BlockSpec(memory_space=pltpu.VMEM), pl.BlockSpec(memory_space=pl.ANY)
+    vmem, smem, hbm = (pl.BlockSpec(memory_space=m) for m in (pltpu.VMEM, pltpu.SMEM, pl.ANY))
     bf16, f32 = jnp.bfloat16, jnp.float32
     dma = pltpu.SemaphoreType.DMA
     out, logs = pl.pallas_call(
@@ -308,9 +335,11 @@
             jax.ShapeDtypeStruct((HEADS, HEAD_DIM), bf16),
             jax.ShapeDtypeStruct((HEADS, 128), f32),
         ],
-        in_specs=[vmem, vmem, vmem, hbm, hbm, hbm, hbm],
+        in_specs=[vmem, smem, smem, hbm, hbm, hbm, hbm],
         out_specs=[vmem, vmem],
         scratch_shapes=[
+            pltpu.VMEM((2, HALF, HEAD_DIM), bf16),
+            pltpu.VMEM((1, 128), f32),
             pltpu.VMEM((rows, HALF, HEAD_DIM), bf16),
             pltpu.VMEM((rows, 1, 128), f32),
             pltpu.VMEM((rows, HALF, HEAD_DIM), f32),
@@ -334,14 +363,14 @@
             pltpu.VMEM((HEADS, 128), f32),
             dma((4,)), dma((3,)), dma((3,)),
             dma((rows,)), dma((rows,)), dma((rows,)), dma((rows,)),
-            dma((count,)), dma((count,)),
+            dma((2, count)), dma((2, count)),
             dma((count,)), dma((count,)), dma((count,)), dma((count,)),
             dma((rows,)), dma((rows,)), dma((rows,)), dma((rows,)),
         ],
         compiler_params=pltpu.CompilerParams(
-            collective_id=0, has_side_effects=True, vmem_limit_bytes=48 * 1024 * 1024
+            collective_id=0, has_side_effects=True, vmem_limit_bytes=63 * 1024 * 1024
         ),
-    )(q, length, position, prefix_keys, prefix_values, suffix_keys, suffix_values)
+    )(queries, prefix_len, block_table, prefix_keys, prefix_values, suffix_keys, suffix_values)
     return out.reshape(1, HEADS * HEAD_DIM), logs[:, 0].reshape(1, HEADS)
 
 

time: 67.9 us -> 57.6 us (0.85)
  Pallas kernels: 59.7 us -> 54.1 us
  local copies, waits for them, and re-layouts: 5.78 us -> 1.97 us
  other arithmetic: 0.79 us -> 0 us
    pallas_call x1, Pallas kernels: 59.7 us -> 54.1 us  [body(): pl.pallas_call(kernel, name='decode', out_shape=[jax.ShapeDtypeStruct((HE...]
    unnamed x11 -> x3, local copies, waits for them, and re-layouts: 5.15 us -> 0.62 us
    slice x1, local copies, waits for them, and re-layouts: 0.63 us -> 1.35 us  [body(): return (out.reshape(1, HEADS * HEAD_DIM), logs[:, 0].reshape(1, HEADS))]
where the time goes in v2:
time: 57.6 us; the launch traced here: 57.4 us
  Pallas kernels  54.1 us (94%)
  local copies, waits for them, and re-layouts  1.97 us (3%)
  between operations  1.29 us (2%)
    pallas_call x1, Pallas kernels, body(): pl.pallas_call(kernel, name='decode', out_shape=[jax.ShapeDtypeStruct((HE...  54.1 us
    slice x1, local copies, waits for them, and re-layouts, body(): return (out.reshape(1, HEADS * HEAD_DIM), logs[:, 0].reshape(1, HEADS))  1.35 us

profile of v2, /device:TPU:1, one launch (start us, length us, event | category | flops | bytes accessed | tf_op | source)
XLA Modules:
  0.0 57.4 jit_solution(13257563305644727639)
XLA Ops:
  1.3 54.1 %decode.1 = (bf16[32,128]{1,0:T(8,128)(2,1)}, f32[32,128]{1,0:T(8,128)}) custom-call(bf16[1,4096]{1,0:T(2,128)(2,1)} %flat_ref.1, s32[1]{0:T(128)S(6)} %copy.12.len_ref, s32[2]{0:T(128)} %table_ref.1, bf16[2,128,2048]{2,1,0:T(8,128)(2,1)} %k_ref.1, bf16[2,128,2048]{2,1,0:T(8,128)(2,1)} %v_ref.1, bf16[1,128,2048]{2,1,0:T(8,128)(2,1)} %ks_ref.1, ...), custom_call_target="tpu_custom_call" | custom-call | tf_op jit(solution)/shard_map/decode/pallas_call | solution.py:331
  55.4 0.0 copy-start
  55.4 1.3 %slice_reduce_fusion = f32[32]{0:T(128)} fusion(f32[32,128]{1,0:T(8,128)} %get-tuple-element.5), kind=kLoop, calls=%fused_computation.1 | loop fusion | bytes 256 | tf_op jit(solution)/shard_map/slice | solution.py:374
  56.8 0.0 copy-done
  56.8 0.6 %copy.11 = bf16[1,1,32,128]{3,1,2,0:T(2,128)(2,1)} copy(bf16[1,1,32,128]{3,2,1,0:T(8,128)(2,1)S(1)} %bitcast.7) | data formatting | bytes 16384
Async XLA Ops:
  55.4 1.4 %copy-start = (bf16[32,128]{1,0:T(8,128)(2,1)S(1)}, bf16[32,128]{1,0:T(8,128)(2,1)}, u32[]{:S(2)}) copy-start(bf16[32,128]{1,0:T(8,128)(2,1)} %get-tuple-element.4) | copy-start | bytes 24580

commit v3 on v2

--- a/solution.py
+++ b/solution.py
@@ -12,9 +12,11 @@
 HEADS = 32
 KV_HEADS = 16
 HEAD_DIM = 128
-HALF = HEADS // 2
-KV_HALF = KV_HEADS // 2
-FIRST = HALF // 2
+TYPES = 4
+LOCAL = HEADS // TYPES
+KV_SET = 2
+PAIR = KV_SET * HEAD_DIM
+FIRST = LOCAL // 2
 AXES = ("x", "y", "z", "c")
 MESH = pl.DeviceIdType.MESH
 
@@ -31,7 +33,7 @@
     flat_ref, len_ref, table_ref, k_ref, v_ref, ks_ref, vs_ref,
     out_ref, log_ref,
     q_ref, own_len, zq, zl, turn, turn2, qg, kbuf, vbuf, pbuf, ksb, vsb,
-    osend, msend, orecv, mrecv, osend2, msend2, orecv2, mrecv2, so, sm, sl,
+    osend, msend, orecv, mrecv, osend2, msend2, orecv2, mrecv2, so, sm, sl, natural,
     local_sem, kv_send, kv_recv, zq_send, zq_recv, zl_send, zl_recv,
     xy_send, xy_recv, ro_send, ro_recv, rm_send, rm_recv,
     fo_send, fo_recv, fm_send, fm_recv,
@@ -41,25 +43,34 @@
     rows = nz * 2
     mine, plane = z * 2 + c, x * ny + y
     other = 1 - c
-    width = KV_HALF * HEAD_DIM
-
-    def columns(half):
-        return pl.ds(pl.multiple_of(half * width, width), width)
-
+    odd = lax.rem(z, 2)
+    pairs = [z + 1 - 2 * odd, lax.rem(z + nz - 1 + 2 * odd, nz)]
+
+    def kind(zz, cc):
+        return lax.rem(zz, 2) * 2 + cc
+
+    def columns(s, t):
+        return pl.ds(pl.multiple_of(s * 8 * HEAD_DIM + t * PAIR, PAIR), PAIR)
+
+    mykind = kind(z, c)
     loads = [
-        pltpu.make_async_copy(k_ref.at[:, :, columns(c)], kbuf.at[0], local_sem.at[0]),
-        pltpu.make_async_copy(v_ref.at[:, :, columns(c)], vbuf.at[0], local_sem.at[1]),
-        pltpu.make_async_copy(ks_ref, ksb, local_sem.at[2]),
-        pltpu.make_async_copy(vs_ref, vsb, local_sem.at[3]),
+        pltpu.make_async_copy(ks_ref, ksb, local_sem.at[0]),
+        pltpu.make_async_copy(vs_ref, vsb, local_sem.at[1]),
     ]
+    for s in range(2):
+        loads += [
+            pltpu.make_async_copy(k_ref.at[:, :, columns(s, mykind)], kbuf.at[s, 0], local_sem.at[2 + s]),
+            pltpu.make_async_copy(v_ref.at[:, :, columns(s, mykind)], vbuf.at[s, 0], local_sem.at[4 + s]),
+        ]
     for load in loads:
         load.start()
 
     flat = flat_ref[...].astype(jnp.float32)
-    for h in range(HEADS):
-        turn2[h % HALF, 0:1, :] = flat[:, h * HEAD_DIM : (h + 1) * HEAD_DIM]
-        if h % HALF == HALF - 1:
-            q_ref[h // HALF] = turn2[:, 0, :].astype(jnp.bfloat16)
+    for t in range(TYPES):
+        for i in range(LOCAL):
+            h = 16 * (i // 4) + 4 * t + i % 4
+            turn2[i, 0:1, :] = flat[:, h * HEAD_DIM : (h + 1) * HEAD_DIM]
+        q_ref[t] = turn2[:, 0, :].astype(jnp.bfloat16)
     own_len[...] = jnp.full((1, 128), len_ref[0], jnp.int32).astype(jnp.float32)
     offset = lax.broadcasted_iota(jnp.int32, (1, 128), 1)
     for b in range(2):
@@ -90,10 +101,10 @@
         return lax.rem(z + nz - dz, nz) * 2 + lax.rem(c + dc, 2)
 
     def line_gather(dz, dc, slot):
-        i, half = dz * 2 + dc, lax.rem(c + dc, 2)
+        i, to = dz * 2 + dc, kind(lax.rem(z + dz, nz), lax.rem(c + dc, 2))
         device = line_id(dz, dc)
         return [
-            remote(q_ref.at[half], zq.at[slot], zq_send.at[i], zq_recv.at[i], device),
+            remote(q_ref.at[to], zq.at[slot], zq_send.at[i], zq_recv.at[i], device),
             remote(own_len, zl.at[slot], zl_send.at[i], zl_recv.at[i], device),
         ]
 
@@ -101,20 +112,30 @@
         for copy in line_gather(dz, dc, mine):
             copy.start()
     partner = {"c": other}
-    swaps = [
-        remote(pbuf.at[0], pbuf.at[1], kv_send.at[0], kv_recv.at[0], partner),
-        remote(k_ref.at[:, :, columns(other)], kbuf.at[1], kv_send.at[1], kv_recv.at[1], partner),
-        remote(v_ref.at[:, :, columns(other)], vbuf.at[1], kv_send.at[2], kv_recv.at[2], partner),
-    ]
+    swaps = [remote(pbuf.at[0], pbuf.at[1], kv_send.at[12], kv_recv.at[12], partner)]
+    for s in range(2):
+        for dc in range(2):
+            i, device = 2 * s + dc, {"z": pairs[s], "c": lax.rem(c + dc, 2)}
+            swaps.append(remote(pbuf.at[0], pbuf.at[2 + i], kv_send.at[13 + i], kv_recv.at[13 + i], device))
+    for ref, buf, at in ((k_ref, kbuf, 0), (v_ref, vbuf, 6)):
+        for s in range(2):
+            source = ref.at[:, :, columns(s, kind(z, other))]
+            swaps.append(remote(source, buf.at[s, 1], kv_send.at[at + s], kv_recv.at[at + s], partner))
+            for dc in range(2):
+                i, core = at + 2 + 2 * s + dc, lax.rem(c + dc, 2)
+                source = ref.at[:, :, columns(s, kind(pairs[s], core))]
+                device = {"z": pairs[s], "c": core}
+                swaps.append(remote(source, buf.at[s, 2 + dc], kv_send.at[i], kv_recv.at[i], device))
     for copy in swaps:
         copy.start()
-    zq[pl.ds(mine, 1)] = q_ref[pl.ds(c, 1)]
+    zq[pl.ds(mine, 1)] = q_ref[pl.ds(mykind, 1)]
     zl[pl.ds(mine, 1)] = own_len[...][None]
 
-    loads[2].wait()
-    loads[3].wait()
+    loads[0].wait()
+    loads[1].wait()
     query = q_ref[...].astype(jnp.float32).reshape(HEADS, HEAD_DIM)
-    head_kv = lax.broadcasted_iota(jnp.int32, (HEADS, HEAD_DIM), 0) // 2
+    place = lax.broadcasted_iota(jnp.int32, (HEADS, HEAD_DIM), 0)
+    head_kv = place % LOCAL // 4 * 8 + place // LOCAL * 2 + place % 4 // 2
     own_scores = jnp.zeros((HEADS, 128), jnp.float32)
     for kv in range(KV_HEADS):
         picked = jnp.where(head_kv == kv, query, 0.0).astype(jnp.bfloat16)
@@ -139,15 +160,15 @@
         for copy in line_gather(dz, dc, line_slot(dz, dc)):
             copy.wait_recv()
     turn[...] = zq[...].astype(jnp.float32)
-    for h in range(HALF):
+    for h in range(LOCAL):
         qg[pl.ds(plane, 1), h] = turn[:, h, :].astype(jnp.bfloat16)[None]
     length = zl[:, 0, :]
     high = jnp.floor(length * (1.0 / 256.0))
     lane = lax.broadcasted_iota(jnp.int32, (rows, 128), 1)
-    qg[pl.ds(plane, 1), HALF] = jnp.where(lane < 64, high, length - high * 256.0).astype(jnp.bfloat16)[None]
+    qg[pl.ds(plane, 1), LOCAL] = jnp.where(lane < 64, high, length - high * 256.0).astype(jnp.bfloat16)[None]
 
     def sheet_pass(colour, bx, by, dx, dy):
-        tiles = pl.ds(0, FIRST) if colour == 0 else pl.ds(FIRST, HALF + 1 - FIRST)
+        tiles = pl.ds(0, FIRST) if colour == 0 else pl.ds(FIRST, LOCAL + 1 - FIRST)
         block = lax.rem(x + bx, nx) * ny + lax.rem(y + by, ny)
         seen = lax.rem(bx + nx - dx, nx) * ny + lax.rem(by + ny - dy, ny)
         sent = (bx + dx) * ny + dy if colour == 0 else dx * ny + by + dy
@@ -157,7 +178,7 @@
         )
 
     def sheet_arrival(colour, bx, by):
-        tiles = pl.ds(0, FIRST) if colour == 0 else pl.ds(FIRST, HALF + 1 - FIRST)
+        tiles = pl.ds(0, FIRST) if colour == 0 else pl.ds(FIRST, LOCAL + 1 - FIRST)
         block = qg.at[lax.rem(x + bx, nx) * ny + lax.rem(y + by, ny), tiles]
         i = bx * ny + by
         return remote(block, block, xy_send.at[colour, i], xy_recv.at[colour, i], sheet_id(0, 0))
@@ -176,14 +197,24 @@
             sheet_pass(*step).start()
         passes += onward
 
-    loads[0].wait()
-    loads[1].wait()
+    for load in loads[2:]:
+        load.wait()
     for copy in swaps:
         copy.wait_recv()
-    positions = jnp.concatenate([pbuf[s, b : b + 1, :] for s in range(2) for b in range(2)], axis=1)
-    tokens = 4 * 128
+    tokens = 8 * 128
+    positions = [
+        jnp.concatenate([pbuf[p, b : b + 1, :] for p in (0, 1, 2 + 2 * s, 3 + 2 * s) for b in range(2)], axis=1)
+        for s in range(2)
+    ]
     ones = jnp.ones((tokens, HEAD_DIM), jnp.bfloat16)
     group = ny * 2 * rows
+    pile = min(rows, 8)
+
+    def packed(tile):
+        tile = tile.reshape(-1, pile, 128)
+        return jnp.stack([
+            jnp.sum(pltpu.roll(tile[i], 0, 1, stride=16, stride_axis=0), axis=0) for i in range(rows // pile)
+        ])
 
     def sheet_return(i, device, here, there):
         return [
@@ -202,19 +233,19 @@
 
         pl.when(k > 0)(arrive)
         base = column * ny
-        tile = qg[pl.ds(base, ny), HALF].astype(jnp.float32)
+        tile = qg[pl.ds(base, ny), LOCAL].astype(jnp.float32)
         wide = tile[:, :, 0:1] * 256.0 + tile[:, :, 64:65]
         limit = jnp.broadcast_to(wide[:, None], (ny, 2, rows, 1)).reshape(group, 1)
-        live = positions < limit
+        live = [position < limit for position in positions]
         lanes = lax.broadcasted_iota(jnp.int32, (ny, rows, 128), 2)
         stats = jnp.zeros((ny, rows, 128), jnp.float32)
-        for g in range(KV_HALF):
-            span = slice(g * HEAD_DIM, (g + 1) * HEAD_DIM)
+        for g in range(2 * KV_SET):
+            s, span = g // KV_SET, slice(g % KV_SET * HEAD_DIM, (g % KV_SET + 1) * HEAD_DIM)
             queries = qg[pl.ds(base, ny), 2 * g : 2 * g + 2].reshape(group, HEAD_DIM)
-            keys = kbuf[:, :, :, span].reshape(tokens, HEAD_DIM)
-            values = vbuf[:, :, :, span].reshape(tokens, HEAD_DIM)
+            keys = kbuf[s, :, :, :, span].reshape(tokens, HEAD_DIM)
+            values = vbuf[s, :, :, :, span].reshape(tokens, HEAD_DIM)
             scores = lax.dot_general(queries, keys, NT, preferred_element_type=jnp.float32) * SCALE2
-            scores = jnp.where(live, scores, MASKED)
+            scores = jnp.where(live[s], scores, MASKED)
             top = jnp.maximum(jnp.max(scores, axis=1, keepdims=True), FLOOR)
             weights = jnp.exp2(scores - top).astype(jnp.bfloat16)
             both = lax.dot_general(
@@ -227,8 +258,9 @@
             sums = both[:, HEAD_DIM:].reshape(ny, 2, rows, 128)
             for j in range(2):
                 stats = jnp.where(lanes == 2 * g + j, tops[:, j], stats)
-                stats = jnp.where(lanes == HALF + 2 * g + j, sums[:, j], stats)
-        msend[pl.ds(base, ny)] = stats
+                stats = jnp.where(lanes == LOCAL + 2 * g + j, sums[:, j], stats)
+        for i in range(ny):
+            msend[pl.ds(base + i, 1)] = packed(stats[i])[None]
         for dy in range(ny):
             row = lax.rem(y + dy, ny)
             there = column * ny + row
@@ -253,30 +285,37 @@
             copy.wait_recv()
     count = nx * ny
     best = jnp.max(mrecv[...], axis=0)
+    at_row = lax.broadcasted_iota(jnp.int32, (rows, 128), 0) % pile * 16
 
     def merge(s, carry):
         total, out = carry
         part = mrecv[pl.ds(s, 1)][0]
         factor = jnp.exp2(part - best)
-        total = total + pltpu.roll(factor, HALF, 1) * part
+        total = total + pltpu.roll(factor, LOCAL, 1) * part
+        spread = jnp.concatenate(
+            [jnp.broadcast_to(factor[i : i + 1], (pile, 128)) for i in range(rows // pile)], axis=0
+        )
         block = orecv[pl.ds(s, 1)][0].astype(jnp.float32)
-        out = tuple(out[h] + factor[:, h : h + 1] * block[h] for h in range(HALF))
+        out = tuple(
+            out[h] + jnp.sum(jnp.where(lane == at_row + h, spread, 0.0), axis=1, keepdims=True) * block[h]
+            for h in range(LOCAL)
+        )
         return total, out
 
     zero = jnp.zeros((rows, HEAD_DIM), jnp.float32)
-    total, out = lax.fori_loop(0, count, merge, (zero, (zero,) * HALF))
-    msend2[:, 0, :] = jnp.where(lane < HALF, best, total)
-    for h in range(HALF):
+    total, out = lax.fori_loop(0, count, merge, (jnp.zeros_like(best), (zero,) * LOCAL))
+    msend2[...] = jnp.where(lane[: rows // pile] % 16 < LOCAL, best, total)
+    for h in range(LOCAL):
         turn2[h] = out[h]
     for r in range(rows):
-        osend2[r] = turn2[:, r, :].astype(jnp.bfloat16)
+        osend2[r] = turn2[:, r, :]
 
     def line_return(dz, dc, here, there):
         i = dz * 2 + dc
         device = line_id(dz, dc)
         return [
             remote(osend2.at[here], orecv2.at[there], fo_send.at[i], fo_recv.at[i], device),
-            remote(msend2.at[here], mrecv2.at[there], fm_send.at[i], fm_recv.at[i], device),
+            remote(msend2, mrecv2.at[there], fm_send.at[i], fm_recv.at[i], device),
         ]
 
     for dz, dc in line:
@@ -284,29 +323,36 @@
         for copy in line_return(dz, dc, target, mine):
             copy.start()
     orecv2[pl.ds(mine, 1)] = osend2[pl.ds(mine, 1)]
-    mrecv2[pl.ds(mine, 1)] = msend2[pl.ds(mine, 1)]
+    mrecv2[pl.ds(mine, 1)] = msend2[...][None]
     for dz, dc in line:
         slot = line_slot(dz, dc)
         for copy in line_return(dz, dc, slot, slot):
             copy.wait_recv()
 
-    lane_of = lax.broadcasted_iota(jnp.int32, (HALF, 128), 1)
-    head_of = lax.broadcasted_iota(jnp.int32, (HALF, 128), 0)
-    for half in range(2):
-        heads = slice(half * HALF, (half + 1) * HALF)
+    lane_of = lax.broadcasted_iota(jnp.int32, (LOCAL, 128), 1)
+    head_of = lax.broadcasted_iota(jnp.int32, (LOCAL, 128), 0)
+    pick = lax.rem(mine, pile) * 16 + head_of
+    for t in range(TYPES):
+        heads = slice(t * LOCAL, (t + 1) * LOCAL)
+        slots = [zz * 2 + t % 2 for zz in range(nz) if zz % 2 == t // 2]
         tops, sums = [sm[heads, 0:1]], [sl[heads, 0:1]]
-        for s in range(nz):
-            row = jnp.broadcast_to(mrecv2[s * 2 + half], (HALF, 128))
-            tops.append(jnp.sum(jnp.where(lane_of == head_of, row, 0.0), axis=1, keepdims=True))
-            sums.append(jnp.sum(jnp.where(lane_of == head_of + HALF, row, 0.0), axis=1, keepdims=True))
+        for slot in slots:
+            row = jnp.broadcast_to(mrecv2[slot, pl.ds(mine // pile, 1), :], (LOCAL, 128))
+            tops.append(jnp.sum(jnp.where(lane_of == pick, row, 0.0), axis=1, keepdims=True))
+            sums.append(jnp.sum(jnp.where(lane_of == pick + LOCAL, row, 0.0), axis=1, keepdims=True))
         top = functools.reduce(jnp.maximum, tops)
-        factors = [jnp.exp2(t - top) for t in tops]
-        normalizer = sum(f * s for f, s in zip(factors, sums))
+        factors = [jnp.exp2(m - top) for m in tops]
+        normalizer = sum(f * l for f, l in zip(factors, sums))
         numerator = factors[0] * so[heads, :]
-        for s in range(nz):
-            numerator += factors[s + 1] * orecv2[s * 2 + half].astype(jnp.float32)
-        out_ref[heads, :] = (numerator / normalizer).astype(jnp.bfloat16)
-        log_ref[heads, :] = jnp.broadcast_to(top * LN2 + jnp.log(normalizer), (HALF, 128))
+        for f, slot in zip(factors[1:], slots):
+            numerator += f * orecv2[slot]
+        numerator = numerator / normalizer
+        logs = jnp.broadcast_to(top * LN2 + jnp.log(normalizer), (LOCAL, 128))
+        for s in range(2):
+            there, here = slice(16 * s + 4 * t, 16 * s + 4 * t + 4), slice(4 * s, 4 * s + 4)
+            natural[there, :] = numerator[here]
+            log_ref[there, :] = logs[here]
+    out_ref[...] = natural[...].astype(jnp.bfloat16)
 
     for copy in swaps:
         copy.wait_send()
@@ -325,6 +371,7 @@
 
 def body(nx, ny, nz, queries, prefix_len, prefix_keys, prefix_values, block_table, suffix_keys, suffix_values):
     rows, count = nz * 2, nx * ny
+    piles = rows // min(rows, 8)
     vmem, smem, hbm = (pl.BlockSpec(memory_space=m) for m in (pltpu.VMEM, pltpu.SMEM, pl.ANY))
     bf16, f32 = jnp.bfloat16, jnp.float32
     dma = pltpu.SemaphoreType.DMA
@@ -338,30 +385,31 @@
         in_specs=[vmem, smem, smem, hbm, hbm, hbm, hbm],
         out_specs=[vmem, vmem],
         scratch_shapes=[
-            pltpu.VMEM((2, HALF, HEAD_DIM), bf16),
+            pltpu.VMEM((TYPES, LOCAL, HEAD_DIM), bf16),
             pltpu.VMEM((1, 128), f32),
-            pltpu.VMEM((rows, HALF, HEAD_DIM), bf16),
+            pltpu.VMEM((rows, LOCAL, HEAD_DIM), bf16),
             pltpu.VMEM((rows, 1, 128), f32),
-            pltpu.VMEM((rows, HALF, HEAD_DIM), f32),
-            pltpu.VMEM((HALF, rows, HEAD_DIM), f32),
-            pltpu.VMEM((count, HALF + 1, rows, HEAD_DIM), bf16),
-            pltpu.VMEM((2, 2, 128, KV_HALF * HEAD_DIM), bf16),
-            pltpu.VMEM((2, 2, 128, KV_HALF * HEAD_DIM), bf16),
-            pltpu.VMEM((2, 8, 128), f32),
+            pltpu.VMEM((rows, LOCAL, HEAD_DIM), f32),
+            pltpu.VMEM((LOCAL, rows, HEAD_DIM), f32),
+            pltpu.VMEM((count, LOCAL + 1, rows, HEAD_DIM), bf16),
+            pltpu.VMEM((2, 4, 2, 128, PAIR), bf16),
+            pltpu.VMEM((2, 4, 2, 128, PAIR), bf16),
+            pltpu.VMEM((6, 8, 128), f32),
             pltpu.VMEM((1, 128, KV_HEADS * HEAD_DIM), bf16),
             pltpu.VMEM((1, 128, KV_HEADS * HEAD_DIM), bf16),
-            pltpu.VMEM((count, HALF, rows, HEAD_DIM), bf16),
-            pltpu.VMEM((count, rows, 128), f32),
-            pltpu.VMEM((count, HALF, rows, HEAD_DIM), bf16),
-            pltpu.VMEM((count, rows, 128), f32),
-            pltpu.VMEM((rows, HALF, HEAD_DIM), bf16),
-            pltpu.VMEM((rows, 1, 128), f32),
-            pltpu.VMEM((rows, HALF, HEAD_DIM), bf16),
-            pltpu.VMEM((rows, 1, 128), f32),
+            pltpu.VMEM((count, LOCAL, rows, HEAD_DIM), bf16),
+            pltpu.VMEM((count, piles, 128), f32),
+            pltpu.VMEM((count, LOCAL, rows, HEAD_DIM), bf16),
+            pltpu.VMEM((count, piles, 128), f32),
+            pltpu.VMEM((rows, LOCAL, HEAD_DIM), f32),
+            pltpu.VMEM((piles, 128), f32),
+            pltpu.VMEM((rows, LOCAL, HEAD_DIM), f32),
+            pltpu.VMEM((rows, piles, 128), f32),
             pltpu.VMEM((HEADS, HEAD_DIM), f32),
             pltpu.VMEM((HEADS, 128), f32),
             pltpu.VMEM((HEADS, 128), f32),
-            dma((4,)), dma((3,)), dma((3,)),
+            pltpu.VMEM((HEADS, HEAD_DIM), f32),
+            dma((6,)), dma((17,)), dma((17,)),
             dma((rows,)), dma((rows,)), dma((rows,)), dma((rows,)),
             dma((2, count)), dma((2, count)),
             dma((count,)), dma((count,)), dma((count,)), dma((count,)),
@@ -374,11 +422,14 @@
     return out.reshape(1, HEADS * HEAD_DIM), logs[:, 0].reshape(1, HEADS)
 
 
+def sizes(mesh):
+    nx = mesh.shape["grp"]
+    nz = 8 if mesh.shape["hold"] == 64 else 2
+    return nx, mesh.shape["hold"] // (2 * nz), nz
+
+
 def solution(mesh):
-    shape = mesh.shape
-    nx = shape["grp"]
-    nz = 8 if shape["hold"] == 64 else 2
-    ny = shape["hold"] // (2 * nz)
+    nx, ny, nz = sizes(mesh)
     split = Mesh(mesh.devices.reshape(nx, ny, nz, 2), AXES)
     rows = P(AXES, None)
     return jax.shard_map(

time: 57.6 us -> 52.9 us (0.918)
  Pallas kernels: 54.1 us -> 49.5 us
    pallas_call x1, Pallas kernels: 54.1 us -> 49.5 us  [body(): pl.pallas_call(kernel, name='decode', out_shape=[jax.ShapeDtypeStruct((HE...]
where the time goes in v3:
time: 52.9 us; the launch traced here: 52.7 us
  Pallas kernels  49.5 us (94%)
  local copies, waits for them, and re-layouts  1.97 us (4%)
  between operations  1.29 us (2%)
    pallas_call x1, Pallas kernels, body(): pl.pallas_call(kernel, name='decode', out_shape=[jax.ShapeDtypeStruct((HE...  49.5 us
    slice x1, local copies, waits for them, and re-layouts, body(): return (out.reshape(1, HEADS * HEAD_DIM), logs[:, 0].reshape(1, HEADS))  1.35 us

profile of v3, /device:TPU:1, one launch (start us, length us, event | category | flops | bytes accessed | tf_op | source)
XLA Modules:
  0.0 52.7 jit_solution(11036894265531377549)
XLA Ops:
  1.3 49.5 %decode.1 = (bf16[32,128]{1,0:T(8,128)(2,1)}, f32[32,128]{1,0:T(8,128)}) custom-call(bf16[1,4096]{1,0:T(2,128)(2,1)} %flat_ref.1, s32[1]{0:T(128)S(6)} %copy.12.len_ref, s32[2]{0:T(128)} %table_ref.1, bf16[2,128,2048]{2,1,0:T(8,128)(2,1)} %k_ref.1, bf16[2,128,2048]{2,1,0:T(8,128)(2,1)} %v_ref.1, bf16[1,128,2048]{2,1,0:T(8,128)(2,1)} %ks_ref.1, ...), custom_call_target="tpu_custom_call" | custom-call | tf_op jit(solution)/shard_map/decode/pallas_call | solution.py:378
  50.7 0.0 copy-start
  50.7 1.3 %slice_reduce_fusion = f32[32]{0:T(128)} fusion(f32[32,128]{1,0:T(8,128)} %get-tuple-element.5), kind=kLoop, calls=%fused_computation.1 | loop fusion | bytes 256 | tf_op jit(solution)/shard_map/slice | solution.py:422
  52.1 0.0 copy-done
  52.1 0.6 %copy.11 = bf16[1,1,32,128]{3,1,2,0:T(2,128)(2,1)} copy(bf16[1,1,32,128]{3,2,1,0:T(8,128)(2,1)S(1)} %bitcast.7) | data formatting | bytes 16384
Async XLA Ops:
  50.7 1.4 %copy-start = (bf16[32,128]{1,0:T(8,128)(2,1)S(1)}, bf16[32,128]{1,0:T(8,128)(2,1)}, u32[]{:S(2)}) copy-start(bf16[32,128]{1,0:T(8,128)(2,1)} %get-tuple-element.4) | copy-start | bytes 24580

commit v4 on v3

v4 whole, which is shorter than its diff:
```python
import functools
import math

import jax
import jax.numpy as jnp
from jax import lax
from jax.experimental import pallas as pl
from jax.experimental.pallas import tpu as pltpu
from jax.sharding import Mesh
from jax.sharding import PartitionSpec as P

HEADS = 32
KV_HEADS = 16
HEAD_DIM = 128
TYPES = 4
LOCAL = HEADS // TYPES
FIRST = LOCAL // 2
AXES = ("x", "y", "z", "c")
MESH = pl.DeviceIdType.MESH

SCALE2 = math.log2(math.e) / 168.0**0.5
LN2 = math.log(2.0)
MASKED = -1e30
FLOOR = -1e29

NT = (((1,), (1,)), ((), ()))
NN = (((1,), (0,)), ((), ()))


def kernel(
    flat_hbm, len_hbm, table_hbm, k_ref, v_ref, ks_ref, vs_ref,
    out_ref, log_ref,
    flat_ref, len_ref, table_ref, q_ref, own_len, zq, zl, turn, turn2, qg, kbuf, vbuf, pbuf, ksb, vsb,
    osend, msend, orecv, mrecv, osend2, msend2, orecv2, mrecv2, so, sm, sl, natural,
    small_sem, local_sem, kv_send, kv_recv, zq_send, zq_recv, zl_send, zl_recv,
    xy_send, xy_recv, ro_send, ro_recv, rm_send, rm_recv,
    fo_send, fo_recv, fm_send, fm_recv,
):
    nx, ny, nz = (lax.axis_size(a) for a in AXES[:3])
    x, y, z, c = (lax.axis_index(a) for a in AXES)
    rows = nz * 2
    mine, plane = z * 2 + c, x * ny + y
    other = 1 - c
    odd = lax.rem(z, 2)
    pairs = [z + 1 - 2 * odd, lax.rem(z + nz - 1 + 2 * odd, nz)]

    def kind(zz, cc):
        return lax.rem(zz, 2) * 2 + cc

    def columns(s, t, e):
        return pl.ds(pl.multiple_of((s * 8 + t * 2 + e) * HEAD_DIM, HEAD_DIM), HEAD_DIM)

    small = [
        pltpu.make_async_copy(src, dst, small_sem.at[i])
        for i, (src, dst) in enumerate([(flat_hbm, flat_ref), (len_hbm, len_ref), (table_hbm, table_ref)])
    ]
    for copy in small:
        copy.start()
    line = [(dz, dc) for dz in range(nz) for dc in range(2) if (dz, dc) != (0, 0)]
    sheet = [(dx, dy) for dx in range(nx) for dy in range(ny) if (dx, dy) != (0, 0)]

    def line_id(dz, dc):
        return {"z": lax.rem(z + dz, nz), "c": lax.rem(c + dc, 2)}

    def sheet_id(dx, dy):
        return {"x": lax.rem(x + dx, nx), "y": lax.rem(y + dy, ny)}

    barrier = pltpu.get_barrier_semaphore()
    for dz, dc in line:
        pl.semaphore_signal(barrier, inc=1, device_id=line_id(dz, dc), device_id_type=MESH)
    for dx, dy in sheet:
        pl.semaphore_signal(barrier, inc=1, device_id=sheet_id(dx, dy), device_id_type=MESH)

    mykind = kind(z, c)
    loads = [
        pltpu.make_async_copy(ks_ref, ksb, local_sem.at[0]),
        pltpu.make_async_copy(vs_ref, vsb, local_sem.at[1]),
    ]
    own = []
    for e in range(2):
        copies = []
        for s in range(2):
            at, span = e * 4 + s * 2 + 2, columns(s, mykind, e)
            copies += [
                pltpu.make_async_copy(k_ref.at[:, :, span], kbuf.at[e, s, 0], local_sem.at[at]),
                pltpu.make_async_copy(v_ref.at[:, :, span], vbuf.at[e, s, 0], local_sem.at[at + 1]),
            ]
        own.append(copies)
        loads = loads + copies
    for load in loads:
        load.start()

    for copy in small:
        copy.wait()
    flat = flat_ref[...].astype(jnp.float32)
    for t in range(TYPES):
        for i in range(LOCAL):
            h = 16 * (i % 4 // 2) + 4 * t + 2 * (i // 4) + i % 2
            turn2[i, 0:1, :] = flat[:, h * HEAD_DIM : (h + 1) * HEAD_DIM]
        q_ref[t] = turn2[:, 0, :].astype(jnp.bfloat16)
    own_len[...] = jnp.full((1, 128), len_ref[0], jnp.int32).astype(jnp.float32)
    offset = lax.broadcasted_iota(jnp.int32, (1, 128), 1)
    for b in range(2):
        pbuf[0, b : b + 1, :] = (table_ref[b] * 128 + offset).astype(jnp.float32)

    pl.semaphore_wait(barrier, len(line) + len(sheet))

    def remote(src, dst, send, recv, device):
        return pltpu.make_async_remote_copy(
            src_ref=src, dst_ref=dst, send_sem=send, recv_sem=recv, device_id=device, device_id_type=MESH
        )

    def line_slot(dz, dc):
        return lax.rem(z + nz - dz, nz) * 2 + lax.rem(c + dc, 2)

    def line_gather(dz, dc, slot):
        i, to = dz * 2 + dc, kind(lax.rem(z + dz, nz), lax.rem(c + dc, 2))
        device = line_id(dz, dc)
        return [
            remote(q_ref.at[to], zq.at[slot], zq_send.at[i], zq_recv.at[i], device),
            remote(own_len, zl.at[slot], zl_send.at[i], zl_recv.at[i], device),
        ]

    for dz, dc in line:
        for copy in line_gather(dz, dc, mine):
            copy.start()
    partner = {"c": other}
    places = [remote(pbuf.at[0], pbuf.at[1], kv_send.at[24], kv_recv.at[24], partner)]
    for s in range(2):
        for dc in range(2):
            i, device = 2 * s + dc, {"z": pairs[s], "c": lax.rem(c + dc, 2)}
            places.append(remote(pbuf.at[0], pbuf.at[2 + i], kv_send.at[25 + i], kv_recv.at[25 + i], device))
    swaps = []
    for e in range(2):
        copies = []
        for ref, buf, at in ((k_ref, kbuf, e * 12), (v_ref, vbuf, e * 12 + 6)):
            for s in range(2):
                for dc in range(2):
                    i, core = at + 2 + 2 * s + dc, lax.rem(c + dc, 2)
                    source = ref.at[:, :, columns(s, kind(pairs[s], core), e)]
                    device = {"z": pairs[s], "c": core}
                    copies.append(remote(source, buf.at[e, s, 2 + dc], kv_send.at[i], kv_recv.at[i], device))
            for s in range(2):
                source = ref.at[:, :, columns(s, kind(z, other), e)]
                copies.append(remote(source, buf.at[e, s, 1], kv_send.at[at + s], kv_recv.at[at + s], partner))
        swaps.append(copies)
    for copy in places + swaps[0] + swaps[1]:
        copy.start()
    zq[pl.ds(mine, 1)] = q_ref[pl.ds(mykind, 1)]
    zl[pl.ds(mine, 1)] = own_len[...][None]

    loads[0].wait()
    loads[1].wait()
    query = q_ref[...].astype(jnp.float32).reshape(HEADS, HEAD_DIM)
    place = lax.broadcasted_iota(jnp.int32, (HEADS, HEAD_DIM), 0)
    head_kv = place % 4 // 2 * 8 + place // LOCAL * 2 + place % LOCAL // 4
    own_scores = jnp.zeros((HEADS, 128), jnp.float32)
    for kv in range(KV_HEADS):
        picked = jnp.where(head_kv == kv, query, 0.0).astype(jnp.bfloat16)
        own_scores += lax.dot_general(
            picked, ksb[0, :, kv * HEAD_DIM : (kv + 1) * HEAD_DIM], NT, preferred_element_type=jnp.float32
        )
    own_scores = own_scores * SCALE2
    own_max = jnp.max(own_scores, axis=1, keepdims=True)
    own_weights = jnp.exp2(own_scores - own_max).astype(jnp.bfloat16)
    own_sum = jnp.sum(own_weights.astype(jnp.float32), axis=1, keepdims=True)
    own_out = jnp.zeros((HEADS, HEAD_DIM), jnp.float32)
    for kv in range(KV_HEADS):
        part = lax.dot_general(
            own_weights, vsb[0, :, kv * HEAD_DIM : (kv + 1) * HEAD_DIM], NN, preferred_element_type=jnp.float32
        )
        own_out += jnp.where(head_kv == kv, part, 0.0)
    so[...] = own_out
    sm[...] = jnp.broadcast_to(own_max, (HEADS, 128))
    sl[...] = jnp.broadcast_to(own_sum, (HEADS, 128))

    for dz, dc in line:
        for copy in line_gather(dz, dc, line_slot(dz, dc)):
            copy.wait_recv()
    turn[...] = zq[...].astype(jnp.float32)
    for h in range(LOCAL):
        qg[pl.ds(plane, 1), h] = turn[:, h, :].astype(jnp.bfloat16)[None]
    length = zl[:, 0, :]
    high = jnp.floor(length * (1.0 / 256.0))
    lane = lax.broadcasted_iota(jnp.int32, (rows, 128), 1)
    qg[pl.ds(plane, 1), LOCAL] = jnp.where(lane < 64, high, length - high * 256.0).astype(jnp.bfloat16)[None]

    def sheet_pass(colour, bx, by, dx, dy):
        tiles = pl.ds(0, FIRST) if colour == 0 else pl.ds(FIRST, LOCAL + 1 - FIRST)
        block = lax.rem(x + bx, nx) * ny + lax.rem(y + by, ny)
        seen = lax.rem(bx + nx - dx, nx) * ny + lax.rem(by + ny - dy, ny)
        sent = (bx + dx) * ny + dy if colour == 0 else dx * ny + by + dy
        return remote(
            qg.at[block, tiles], qg.at[block, tiles],
            xy_send.at[colour, sent], xy_recv.at[colour, seen], sheet_id(dx, dy),
        )

    def sheet_arrival(colour, bx, by):
        tiles = pl.ds(0, FIRST) if colour == 0 else pl.ds(FIRST, LOCAL + 1 - FIRST)
        block = qg.at[lax.rem(x + bx, nx) * ny + lax.rem(y + by, ny), tiles]
        i = bx * ny + by
        return remote(block, block, xy_send.at[colour, i], xy_recv.at[colour, i], sheet_id(0, 0))

    along_x = [1 + (i // 2 if i % 2 == 0 else nx - 2 - i // 2) for i in range(nx - 1)]
    along_y = [1 + (i // 2 if i % 2 == 0 else ny - 2 - i // 2) for i in range(ny - 1)]
    passes = [(0, 0, 0, dx, 0) for dx in along_x] + [(1, 0, 0, 0, dy) for dy in along_y]
    passes += [(0, 0, 0, 0, dy) for dy in along_y] + [(1, 0, 0, dx, 0) for dx in along_x]
    for step in passes:
        sheet_pass(*step).start()
    seen_first = [(0, bx, 0) for bx in along_x] + [(1, 0, by) for by in along_y]
    for colour, bx, by in sorted(seen_first, key=lambda b: (along_x + along_y).index(b[1] + b[2])):
        sheet_arrival(colour, bx, by).wait_recv()
        onward = [(0, bx, 0, 0, dy) for dy in along_y] if colour == 0 else [(1, 0, by, dx, 0) for dx in along_x]
        for step in onward:
            sheet_pass(*step).start()
        passes += onward

    for copy in places:
        copy.wait_recv()
    tokens = 8 * 128
    positions = [
        jnp.concatenate([pbuf[p, b : b + 1, :] for p in (0, 1, 2 + 2 * s, 3 + 2 * s) for b in range(2)], axis=1)
        for s in range(2)
    ]
    ones = jnp.ones((tokens, HEAD_DIM), jnp.bfloat16)
    group = ny * 2 * rows
    pile = min(rows, 8)

    def packed(tile):
        tile = tile.reshape(-1, pile, 128)
        line = sum(pltpu.roll(tile[i], 64 * i, 1, stride=8, stride_axis=0) for i in range(rows // pile))
        return jnp.sum(line, axis=0, keepdims=True)

    def sheet_return(e, i, device, here, there):
        return [
            remote(osend.at[e, here], orecv.at[e, there], ro_send.at[e, i], ro_recv.at[e, i], device),
            remote(msend.at[e, here], mrecv.at[e, there], rm_send.at[e, i], rm_recv.at[e, i], device),
        ]

    def chunk(e, k):
        column = lax.rem(x + k, nx)
        base = column * ny
        if e == 0:
            for dy in range(1, ny):
                sheet_arrival(0, k, dy).wait_recv()

            def arrive():
                for dy in range(ny):
                    sheet_arrival(1, k, dy).wait_recv()

            pl.when(k > 0)(arrive)
        tile = qg[pl.ds(base, ny), LOCAL].astype(jnp.float32)
        wide = tile[:, :, 0:1] * 256.0 + tile[:, :, 64:65]
        limit = jnp.broadcast_to(wide[:, None], (ny, 2, rows, 1)).reshape(group, 1)
        lanes = lax.broadcasted_iota(jnp.int32, (ny, rows, 128), 2)
        stats = jnp.zeros((ny, rows, 128), jnp.float32)
        for s in range(2):
            g = 2 * e + s
            queries = qg[pl.ds(base, ny), 2 * g : 2 * g + 2].reshape(group, HEAD_DIM)
            keys = kbuf[e, s].reshape(tokens, HEAD_DIM)
            values = vbuf[e, s].reshape(tokens, HEAD_DIM)
            scores = lax.dot_general(queries, keys, NT, preferred_element_type=jnp.float32) * SCALE2
            scores = jnp.where(positions[s] < limit, scores, MASKED)
            top = jnp.maximum(jnp.max(scores, axis=1, keepdims=True), FLOOR)
            weights = jnp.exp2(scores - top).astype(jnp.bfloat16)
            both = lax.dot_general(
                weights, jnp.concatenate([values, ones], axis=1), NN, preferred_element_type=jnp.float32
            )
            osend[e, pl.ds(base, ny), 2 * s : 2 * s + 2] = (
                both[:, :HEAD_DIM].astype(jnp.bfloat16).reshape(ny, 2, rows, HEAD_DIM)
            )
            tops = jnp.broadcast_to(top, (group, 128)).reshape(ny, 2, rows, 128)
            sums = both[:, HEAD_DIM:].reshape(ny, 2, rows, 128)
            for j in range(2):
                stats = jnp.where(lanes == 2 * s + j, tops[:, j], stats)
                stats = jnp.where(lanes == 4 + 2 * s + j, sums[:, j], stats)
        for i in range(ny):
            msend[e, pl.ds(base + i, 1)] = packed(stats[i])[None]
        for dy in range(ny):
            row = lax.rem(y + dy, ny)
            there = column * ny + row

            def leave(dy=dy, row=row, there=there):
                for copy in sheet_return(e, k * ny + dy, {"x": column, "y": row}, there, plane):
                    copy.start()

            if dy == 0:
                pl.when(k > 0)(leave)
            else:
                leave()

    for e in range(2):
        for copy in own[e]:
            copy.wait()
        for copy in swaps[e]:
            copy.wait_recv()
        lax.fori_loop(0, nx, lambda k, carry, e=e: (chunk(e, lax.rem(k + e, nx)), carry)[1], 0)
        orecv[e, pl.ds(plane, 1)] = osend[e, pl.ds(plane, 1)]
        mrecv[e, pl.ds(plane, 1)] = msend[e, pl.ds(plane, 1)]

    def line_return(e, dz, dc, here, there):
        i = dz * 2 + dc
        device = line_id(dz, dc)
        return [
            remote(osend2.at[e, here], orecv2.at[e, there], fo_send.at[e, i], fo_recv.at[e, i], device),
            remote(msend2.at[e], mrecv2.at[e, there], fm_send.at[e, i], fm_recv.at[e, i], device),
        ]

    count = nx * ny
    at_row = lax.broadcasted_iota(jnp.int32, (rows, 128), 0) * 8
    zero = jnp.zeros((rows, HEAD_DIM), jnp.float32)
    for e in range(2):
        for dx, dy in sheet:
            slot = lax.rem(x + nx - dx, nx) * ny + lax.rem(y + ny - dy, ny)
            for copy in sheet_return(e, dx * ny + dy, sheet_id(dx, dy), slot, slot):
                copy.wait_recv()
        best = jnp.max(mrecv[e], axis=0)

        def merge(s, carry, e=e, best=best):
            total, out = carry
            part = mrecv[e, pl.ds(s, 1)][0]
            factor = jnp.exp2(part - best)
            total = total + pltpu.roll(factor, 4, 1) * part
            spread = jnp.broadcast_to(factor, (rows, 128))
            block = orecv[e, pl.ds(s, 1)][0].astype(jnp.float32)
            out = tuple(
                out[h] + jnp.sum(jnp.where(lane == at_row + h, spread, 0.0), axis=1, keepdims=True) * block[h]
                for h in range(4)
            )
            return total, out

        total, out = lax.fori_loop(0, count, merge, (jnp.zeros_like(best), (zero,) * 4), unroll=4)
        msend2[e] = jnp.where(lane[:1] % 8 < 4, best, total)
        for h in range(4):
            turn2[4 * e + h] = out[h]
        for r in range(rows):
            osend2[e, r] = turn2[4 * e : 4 * e + 4, r, :]
        for dz, dc in line:
            target = lax.rem(z + dz, nz) * 2 + lax.rem(c + dc, 2)
            for copy in line_return(e, dz, dc, target, mine):
                copy.start()
        orecv2[e, pl.ds(mine, 1)] = osend2[e, pl.ds(mine, 1)]
        mrecv2[e, pl.ds(mine, 1)] = msend2[e][None]

    lane_of = lax.broadcasted_iota(jnp.int32, (4, 128), 1)
    line_log = jnp.zeros((1, 128), jnp.float32)
    head_row = lax.broadcasted_iota(jnp.int32, (4, 128), 0)
    pick = mine * 8 + lax.broadcasted_iota(jnp.int32, (4, 128), 0)
    for e in range(2):
        for dz, dc in line:
            slot = line_slot(dz, dc)
            for copy in line_return(e, dz, dc, slot, slot):
                copy.wait_recv()
        for t in range(TYPES):
            heads = slice(t * LOCAL + 4 * e, t * LOCAL + 4 * e + 4)
            slots = [zz * 2 + t % 2 for zz in range(nz) if zz % 2 == t // 2]
            tops, sums = [sm[heads, 0:1]], [sl[heads, 0:1]]
            for slot in slots:
                row = jnp.broadcast_to(mrecv2[e, slot], (4, 128))
                tops.append(jnp.sum(jnp.where(lane_of == pick, row, 0.0), axis=1, keepdims=True))
                sums.append(jnp.sum(jnp.where(lane_of == pick + 4, row, 0.0), axis=1, keepdims=True))
            top = functools.reduce(jnp.maximum, tops)
            factors = [jnp.exp2(m - top) for m in tops]
            normalizer = sum(f * l for f, l in zip(factors, sums))
            numerator = factors[0] * so[heads, :]
            for f, slot in zip(factors[1:], slots):
                numerator += f * orecv2[e, slot]
            numerator = numerator / normalizer
            logs = jnp.broadcast_to(top * LN2 + jnp.log(normalizer), (4, 128))
            wanted = 16 * (head_row // 2) + 4 * t + 2 * e + head_row % 2
            line_log += jnp.sum(jnp.where(lane_of == wanted, logs, 0.0), axis=0, keepdims=True)
            for s in range(2):
                first = 16 * s + 4 * t + 2 * e
                natural[first : first + 2, :] = numerator[2 * s : 2 * s + 2]
    for h in range(HEADS):
        out_ref[:, h * HEAD_DIM : (h + 1) * HEAD_DIM] = natural[h : h + 1, :].astype(jnp.bfloat16)
    log_ref[...] = line_log[:, :HEADS]

    for copy in places + swaps[0] + swaps[1]:
        copy.wait_send()
    for step in passes:
        sheet_pass(*step).wait_send()
    for dz, dc in line:
        target = lax.rem(z + dz, nz) * 2 + lax.rem(c + dc, 2)
        for copy in line_gather(dz, dc, mine):
            copy.wait_send()
        for e in range(2):
            for copy in line_return(e, dz, dc, target, mine):
                copy.wait_send()
    for dx, dy in sheet:
        i, device = dx * ny + dy, sheet_id(dx, dy)
        there = lax.rem(x + dx, nx) * ny + lax.rem(y + dy, ny)
        for e in range(2):
            for copy in sheet_return(e, i, device, there, plane):
                copy.wait_send()


def body(nx, ny, nz, queries, prefix_len, prefix_keys, prefix_values, block_table, suffix_keys, suffix_values):
    rows, count = nz * 2, nx * ny
    vmem, hbm = pl.BlockSpec(memory_space=pltpu.VMEM), pl.BlockSpec(memory_space=pltpu.HBM)
    bf16, f32 = jnp.bfloat16, jnp.float32
    dma = pltpu.SemaphoreType.DMA
    out, logs = pl.pallas_call(
        kernel,
        name="decode",
        out_shape=[
            jax.ShapeDtypeStruct((1, HEADS * HEAD_DIM), bf16),
            jax.ShapeDtypeStruct((1, HEADS), f32),
        ],
        in_specs=[hbm, hbm, hbm, hbm, hbm, hbm, hbm],
        out_specs=[vmem, vmem],
        scratch_shapes=[
            pltpu.VMEM((1, HEADS * HEAD_DIM), bf16),
            pltpu.SMEM((1,), jnp.int32),
            pltpu.SMEM((2,), jnp.int32),
            pltpu.VMEM((TYPES, LOCAL, HEAD_DIM), bf16),
            pltpu.VMEM((1, 128), f32),
            pltpu.VMEM((rows, LOCAL, HEAD_DIM), bf16),
            pltpu.VMEM((rows, 1, 128), f32),
            pltpu.VMEM((rows, LOCAL, HEAD_DIM), f32),
            pltpu.VMEM((LOCAL, rows, HEAD_DIM), f32),
            pltpu.VMEM((count, LOCAL + 1, rows, HEAD_DIM), bf16),
            pltpu.VMEM((2, 2, 4, 2, 128, HEAD_DIM), bf16),
            pltpu.VMEM((2, 2, 4, 2, 128, HEAD_DIM), bf16),
            pltpu.VMEM((6, 8, 128), f32),
            pltpu.VMEM((1, 128, KV_HEADS * HEAD_DIM), bf16),
            pltpu.VMEM((1, 128, KV_HEADS * HEAD_DIM), bf16),
            pltpu.VMEM((2, count, 4, rows, HEAD_DIM), bf16),
            pltpu.VMEM((2, count, 1, 128), f32),
            pltpu.VMEM((2, count, 4, rows, HEAD_DIM), bf16),
            pltpu.VMEM((2, count, 1, 128), f32),
            pltpu.VMEM((2, rows, 4, HEAD_DIM), f32),
            pltpu.VMEM((2, 1, 128), f32),
            pltpu.VMEM((2, rows, 4, HEAD_DIM), f32),
            pltpu.VMEM((2, rows, 1, 128), f32),
            pltpu.VMEM((HEADS, HEAD_DIM), f32),
            pltpu.VMEM((HEADS, 128), f32),
            pltpu.VMEM((HEADS, 128), f32),
            pltpu.VMEM((HEADS, HEAD_DIM), f32),
            dma((3,)), dma((10,)), dma((29,)), dma((29,)),
            dma((rows,)), dma((rows,)), dma((rows,)), dma((rows,)),
            dma((2, count)), dma((2, count)),
            dma((2, count)), dma((2, count)), dma((2, count)), dma((2, count)),
            dma((2, rows)), dma((2, rows)), dma((2, rows)), dma((2, rows)),
        ],
        compiler_params=pltpu.CompilerParams(
            collective_id=0, has_side_effects=True, vmem_limit_bytes=63 * 1024 * 1024
        ),
    )(queries, prefix_len, block_table, prefix_keys, prefix_values, suffix_keys, suffix_values)
    return out, logs


def sizes(mesh):
    nx = mesh.shape["grp"]
    nz = 8 if mesh.shape["hold"] == 64 else 2
    return nx, mesh.shape["hold"] // (2 * nz), nz


def solution(mesh):
    nx, ny, nz = sizes(mesh)
    split = Mesh(mesh.devices.reshape(nx, ny, nz, 2), AXES)
    rows = P(AXES, None)
    return jax.shard_map(
        functools.partial(body, nx, ny, nz),
        mesh=split,
        in_specs=(rows, P(AXES), P(AXES, None, None), P(AXES, None, None), P(AXES), P(AXES, None, None), P(AXES, None, None)),
        out_specs=(rows, rows),
        check_vma=False,
    )
```

time: 52.9 us -> 47.8 us (0.904)
  Pallas kernels: 49.5 us -> 44.5 us
    pallas_call x1, Pallas kernels: 49.5 us -> 44.5 us  [body(): pl.pallas_call(kernel, name='decode', out_shape=[jax.ShapeDtypeStruct((1,...]
    slice x1 -> x0, local copies, waits for them, and re-layouts: 1.35 us -> none  [body(): return (out.reshape(1, HEADS * HEAD_DIM), logs[:, 0].reshape(1, HEADS))]
    unnamed x3 -> x4, local copies, waits for them, and re-layouts: 0.62 us -> 1.85 us
where the time goes in v4:
time: 47.8 us; the launch traced here: 47.6 us
  Pallas kernels  44.5 us (93%)
  local copies, waits for them, and re-layouts  1.85 us (4%)
  between operations  1.29 us (3%)
    pallas_call x1, Pallas kernels, body(): pl.pallas_call(kernel, name='decode', out_shape=[jax.ShapeDtypeStruct((1,...  44.5 us
    unnamed x4, local copies, waits for them, and re-layouts  1.85 us

profile of v4, /device:TPU:1, one launch (start us, length us, event | category | flops | bytes accessed | tf_op | source)
XLA Modules:
  0.0 47.6 jit_solution(10205459735281700467)
XLA Ops:
  1.3 44.5 %decode.1 = (bf16[1,4096]{1,0:T(2,128)(2,1)}, f32[1,32]{1,0:T(1,128)}) custom-call(bf16[1,4096]{1,0:T(2,128)(2,1)} %flat_hbm.1, s32[1]{0:T(128)S(6)} %copy.11.len_hbm, s32[2]{0:T(128)} %table_hbm.1, bf16[2,128,2048]{2,1,0:T(8,128)(2,1)} %k_ref.1, bf16[2,128,2048]{2,1,0:T(8,128)(2,1)} %v_ref.1, bf16[1,128,2048]{2,1,0:T(8,128)(2,1)} %ks_ref.1, ...), custom_call_target="tpu_custom_call" | custom-call | tf_op jit(solution)/shard_map/decode/pallas_call | solution.py:403
  45.7 0.0 copy-start
  45.7 1.3 %copy.12 = bf16[1,4096]{1,0:T(2,128)(2,1)} copy(bf16[1,4096]{1,0:T(2,128)(2,1)} %get-tuple-element.4) | data formatting | bytes 16384
  47.1 0.0 copy-done
  47.1 0.5 %copy.13 = f32[1,32]{1,0:T(1,128)} copy(f32[1,32]{1,0:T(1,128)S(1)} %copy-done) | data formatting | bytes 256
Async XLA Ops:
  45.7 1.4 %copy-start = (f32[1,32]{1,0:T(1,128)S(1)}, f32[1,32]{1,0:T(1,128)}, u32[]{:S(2)}) copy-start(f32[1,32]{1,0:T(1,128)} %get-tuple-element.5) | copy-start | bytes 388

commit v5 on v4

--- a/solution.py
+++ b/solution.py
@@ -57,7 +57,9 @@
     for copy in small:
         copy.start()
     line = [(dz, dc) for dz in range(nz) for dc in range(2) if (dz, dc) != (0, 0)]
+    line.sort(key=lambda d: -min(d[0], nz - d[0]))
     sheet = [(dx, dy) for dx in range(nx) for dy in range(ny) if (dx, dy) != (0, 0)]
+    sheet.sort(key=lambda d: -min(d[0], nx - d[0]) - min(d[1], ny - d[1]))
 
     def line_id(dz, dc):
         return {"z": lax.rem(z + dz, nz), "c": lax.rem(c + dc, 2)}
@@ -341,6 +343,24 @@
                 copy.start()
         orecv2[e, pl.ds(mine, 1)] = osend2[e, pl.ds(mine, 1)]
         mrecv2[e, pl.ds(mine, 1)] = msend2[e][None]
+
+    for copy in places + swaps[0] + swaps[1]:
+        copy.wait_send()
+    for step in passes:
+        sheet_pass(*step).wait_send()
+    for dz, dc in line:
+        target = lax.rem(z + dz, nz) * 2 + lax.rem(c + dc, 2)
+        for copy in line_gather(dz, dc, mine):
+            copy.wait_send()
+        for e in range(2):
+            for copy in line_return(e, dz, dc, target, mine):
+                copy.wait_send()
+    for dx, dy in sheet:
+        i, device = dx * ny + dy, sheet_id(dx, dy)
+        there = lax.rem(x + dx, nx) * ny + lax.rem(y + dy, ny)
+        for e in range(2):
+            for copy in sheet_return(e, i, device, there, plane):
+                copy.wait_send()
 
     lane_of = lax.broadcasted_iota(jnp.int32, (4, 128), 1)
     line_log = jnp.zeros((1, 128), jnp.float32)
@@ -376,23 +396,10 @@
         out_ref[:, h * HEAD_DIM : (h + 1) * HEAD_DIM] = natural[h : h + 1, :].astype(jnp.bfloat16)
     log_ref[...] = line_log[:, :HEADS]
 
-    for copy in places + swaps[0] + swaps[1]:
-        copy.wait_send()
-    for step in passes:
-        sheet_pass(*step).wait_send()
-    for dz, dc in line:
-        target = lax.rem(z + dz, nz) * 2 + lax.rem(c + dc, 2)
-        for copy in line_gather(dz, dc, mine):
-            copy.wait_send()
-        for e in range(2):
-            for copy in line_return(e, dz, dc, target, mine):
-                copy.wait_send()
-    for dx, dy in sheet:
-        i, device = dx * ny + dy, sheet_id(dx, dy)
-        there = lax.rem(x + dx, nx) * ny + lax.rem(y + dy, ny)
-        for e in range(2):
-            for copy in sheet_return(e, i, device, there, plane):
-                copy.wait_send()
+
+def settle(out_ref, log_ref, out_final, log_final):
+    out_final[...] = out_ref[...]
+    log_final[...] = log_ref[...]
 
 
 def body(nx, ny, nz, queries, prefix_len, prefix_keys, prefix_values, block_table, suffix_keys, suffix_values):
@@ -404,8 +411,8 @@
         kernel,
         name="decode",
         out_shape=[
-            jax.ShapeDtypeStruct((1, HEADS * HEAD_DIM), bf16),
-            jax.ShapeDtypeStruct((1, HEADS), f32),
+            pltpu.VMEM((1, HEADS * HEAD_DIM), bf16),
+            pltpu.VMEM((1, HEADS), f32),
         ],
         in_specs=[hbm, hbm, hbm, hbm, hbm, hbm, hbm],
         out_specs=[vmem, vmem],
@@ -447,7 +454,13 @@
             collective_id=0, has_side_effects=True, vmem_limit_bytes=63 * 1024 * 1024
         ),
     )(queries, prefix_len, block_table, prefix_keys, prefix_values, suffix_keys, suffix_values)
-    return out, logs
+    return tuple(pl.pallas_call(
+        settle,
+        name="settle",
+        out_shape=[jax.ShapeDtypeStruct(out.shape, bf16), jax.ShapeDtypeStruct(logs.shape, f32)],
+        in_specs=[vmem, vmem],
+        out_specs=[vmem, vmem],
+    )(*(pltpu.with_memory_space_constraint(a, pltpu.VMEM) for a in (out, logs))))
 
 
 def sizes(mesh):

time: 47.8 us -> 45.3 us (0.948)
  local copies, waits for them, and re-layouts: 1.85 us -> 0 us
  Pallas kernels: 44.5 us -> 43.8 us
    unnamed x4 -> x0, local copies, waits for them, and re-layouts: 1.85 us -> none
    pallas_call x1 -> x2, Pallas kernels: 44.5 us -> 43.8 us  [the longest x1 43.2 us: body(): pl.pallas_call(kernel, name='decode', out_shape=[pltpu.VMEM((1, HEADS * H...]
where the time goes in v5:
time: 45.3 us; the launch traced here: 45.1 us
  Pallas kernels  43.8 us (97%)
  between operations  1.28 us (3%)
    pallas_call x1, Pallas kernels, body(): pl.pallas_call(kernel, name='decode', out_shape=[pltpu.VMEM((1, HEADS * H...  43.2 us

profile of v5, /device:TPU:1, one launch (start us, length us, event | category | flops | bytes accessed | tf_op | source)
XLA Modules:
  0.0 45.1 jit_solution(7981142958763039970)
XLA Ops:
  1.3 43.2 %decode.1 = (bf16[1,4096]{1,0:T(2,128)(2,1)S(1)}, f32[1,32]{1,0:T(1,128)S(1)}) custom-call(bf16[1,4096]{1,0:T(2,128)(2,1)} %flat_hbm.1, s32[1]{0:T(128)S(6)} %copy.9.len_hbm, s32[2]{0:T(128)} %table_hbm.1, bf16[2,128,2048]{2,1,0:T(8,128)(2,1)} %k_ref.1, bf16[2,128,2048]{2,1,0:T(8,128)(2,1)} %v_ref.1, bf16[1,128,2048]{2,1,0:T(8,128)(2,1)} %ks_ref.1, ...), custom_call_target="tpu_custom_call" | custom-call | tf_op jit(solution)/shard_map/decode/pallas_call | solution.py:410
  44.5 0.6 %settle.1 = (bf16[1,4096]{1,0:T(2,128)(2,1)}, f32[1,32]{1,0:T(1,128)}) custom-call(bf16[1,4096]{1,0:T(2,128)(2,1)S(1)} %get-tuple-element.4.out_ref, f32[1,32]{1,0:T(1,128)S(1)} %get-tuple-element.5.log_ref), custom_call_target="tpu_custom_call" | custom-call | tf_op jit(solution)/shard_map/settle/pallas_call | solution.py:457

commit v6 on v5

--- a/solution.py
+++ b/solution.py
@@ -205,12 +205,15 @@
 
     along_x = [1 + (i // 2 if i % 2 == 0 else nx - 2 - i // 2) for i in range(nx - 1)]
     along_y = [1 + (i // 2 if i % 2 == 0 else ny - 2 - i // 2) for i in range(ny - 1)]
+    near_first = along_x + along_y
+    along_x.sort(key=lambda d: -min(d, nx - d))
+    along_y.sort(key=lambda d: -min(d, ny - d))
     passes = [(0, 0, 0, dx, 0) for dx in along_x] + [(1, 0, 0, 0, dy) for dy in along_y]
     passes += [(0, 0, 0, 0, dy) for dy in along_y] + [(1, 0, 0, dx, 0) for dx in along_x]
     for step in passes:
         sheet_pass(*step).start()
     seen_first = [(0, bx, 0) for bx in along_x] + [(1, 0, by) for by in along_y]
-    for colour, bx, by in sorted(seen_first, key=lambda b: (along_x + along_y).index(b[1] + b[2])):
+    for colour, bx, by in sorted(seen_first, key=lambda b: near_first.index(b[1] + b[2])):
         sheet_arrival(colour, bx, by).wait_recv()
         onward = [(0, bx, 0, 0, dy) for dy in along_y] if colour == 0 else [(1, 0, by, dx, 0) for dx in along_x]
         for step in onward:
@@ -278,7 +281,7 @@
                 stats = jnp.where(lanes == 4 + 2 * s + j, sums[:, j], stats)
         for i in range(ny):
             msend[e, pl.ds(base + i, 1)] = packed(stats[i])[None]
-        for dy in range(ny):
+        for dy in sorted(range(ny), key=lambda d: -min(d, ny - d)):
             row = lax.rem(y + dy, ny)
             there = column * ny + row
 

time: 45.3 us -> 44.9 us (level)
  no operation moved by 1% of the time
where the time goes in v6:
time: 44.9 us; the launch traced here: 44.8 us
  Pallas kernels  43.5 us (97%)
  between operations  1.28 us (3%)
    pallas_call x1, Pallas kernels, body(): pl.pallas_call(kernel, name='decode', out_shape=[pltpu.VMEM((1, HEADS * H...  42.8 us

profile of v6, /device:TPU:1, one launch (start us, length us, event | category | flops | bytes accessed | tf_op | source)
XLA Modules:
  0.0 44.8 jit_solution(15999641212586813744)
XLA Ops:
  1.3 42.8 %decode.1 = (bf16[1,4096]{1,0:T(2,128)(2,1)S(1)}, f32[1,32]{1,0:T(1,128)S(1)}) custom-call(bf16[1,4096]{1,0:T(2,128)(2,1)} %flat_hbm.1, s32[1]{0:T(128)S(6)} %copy.9.len_hbm, s32[2]{0:T(128)} %table_hbm.1, bf16[2,128,2048]{2,1,0:T(8,128)(2,1)} %k_ref.1, bf16[2,128,2048]{2,1,0:T(8,128)(2,1)} %v_ref.1, bf16[1,128,2048]{2,1,0:T(8,128)(2,1)} %ks_ref.1, ...), custom_call_target="tpu_custom_call" | custom-call | tf_op jit(solution)/shard_map/decode/pallas_call | solution.py:413
  44.1 0.6 %settle.1 = (bf16[1,4096]{1,0:T(2,128)(2,1)}, f32[1,32]{1,0:T(1,128)}) custom-call(bf16[1,4096]{1,0:T(2,128)(2,1)S(1)} %get-tuple-element.4.out_ref, f32[1,32]{1,0:T(1,128)S(1)} %get-tuple-element.5.log_ref), custom_call_target="tpu_custom_call" | custom-call | tf_op jit(solution)/shard_map/settle/pallas_call | solution.py:460
